TPU v7x, 32 devices: a whole 2x2x4 slice. The times are simulated.
32 devices in a mesh: hp: 4 (over z), cp: 8 (over y, x, core).
Axes of the slice: x: 2, y: 2, z: 4, core: 2. Of those that a mesh axis runs over, the one named last changes fastest.
Arguments:
- hidden: bfloat16 [4096, 3072], P(('cp', 'hp'))
- grad_out: bfloat16 [4096, 3072], P(('cp', 'hp'))
- positions: int32 [4096], P(('cp', 'hp'))
- norm_gain: bfloat16 [3072], replicated
- w_q: bfloat16 [3072, 3072], replicated
- w_k: bfloat16 [3072, 1024], replicated
- w_v: bfloat16 [3072, 1024], replicated
- w_o: bfloat16 [3072, 3072], replicated
- inv_freq: float32 [64], replicated
Outputs:
- output 1: bfloat16 [4096, 3072], P(('cp', 'hp'))
- output 2: bfloat16 [4096, 3072], P(('cp', 'hp'))
- output 3: float32 [3072, 3072], replicated
- output 4: float32 [3072, 1024], replicated
- output 5: float32 [3072, 1024], replicated
- output 6: float32 [3072, 3072], replicated
- output 7: float32 [3072], replicated
All inputs are finite; a program needn't handle non-finite values.
Results may differ from a plain program's by a relative error of at most 0.0123283.
Values are sent between devices in bfloat16 or wider.
A program may use at most 1 GiB of HBM per device.

v0:
```python
import jax
import jax.numpy as jnp
from jax import lax
from jax.sharding import PartitionSpec as P

NORM_EPS = 1e-5


def rope_apply(vectors, cos_t, sin_t):
    half_dim = vectors.shape[-1] // 2
    lo_half = vectors[..., :half_dim]
    hi_half = vectors[..., half_dim:]
    return jnp.concatenate([lo_half * cos_t - hi_half * sin_t, hi_half * cos_t + lo_half * sin_t], axis=-1)


def rope_undo(vectors, cos_t, sin_t):
    half_dim = vectors.shape[-1] // 2
    lo_half = vectors[..., :half_dim]
    hi_half = vectors[..., half_dim:]
    return jnp.concatenate([lo_half * cos_t + hi_half * sin_t, hi_half * cos_t - lo_half * sin_t], axis=-1)


def pair_index(pair_id, n_pairs, pair_rows):
    block_len = pair_rows // 2
    within = jnp.arange(pair_rows, dtype=jnp.int32)
    return jnp.where(within < block_len, pair_id * block_len + within, (2 * n_pairs - 1 - pair_id) * block_len + within - block_len)


def stored_index(n_pairs, pair_rows):
    block_len = pair_rows // 2
    rows_idx = jnp.arange(n_pairs * pair_rows, dtype=jnp.int32)
    pair_id = rows_idx // pair_rows
    within = rows_idx % pair_rows
    return jnp.where(within < block_len, pair_id * block_len + within, (2 * n_pairs - 1 - pair_id) * block_len + within - block_len)


def solution(mesh):
    hp_size = mesh.shape['hp']
    cp_size = mesh.shape['cp']

    def device_step(hidden, grad_out, positions, norm_gain, w_q, w_k, w_v, w_o, inv_freq):
        tok_rows = hidden.shape[0]
        head_dim = 2 * inv_freq.shape[0]
        n_heads = w_q.shape[1] // head_dim
        n_kv = w_k.shape[1] // head_dim
        repeat = max(1, hp_size // n_kv)
        loc_heads = n_heads // hp_size
        loc_kv = n_kv * repeat // hp_size
        loc_group = loc_heads // loc_kv
        pair_rows = tok_rows * hp_size
        score_scale = head_dim ** -0.5
        cp_idx = lax.axis_index('cp')
        x_f32 = hidden.astype(jnp.float32)
        inv_rms = lax.rsqrt(jnp.mean(x_f32 * x_f32, axis=-1, keepdims=True) + NORM_EPS)
        x_hat = x_f32 * inv_rms
        normed = (x_hat * norm_gain.astype(jnp.float32)).astype(jnp.bfloat16)
        angles = positions.astype(jnp.float32)[:, None] * inv_freq[None, :]
        cos_t = jnp.cos(angles)[:, None, :]
        sin_t = jnp.sin(angles)[:, None, :]
        q_rot = rope_apply(jnp.dot(normed, w_q, preferred_element_type=jnp.float32).reshape(tok_rows, n_heads, head_dim), cos_t, sin_t).astype(jnp.bfloat16)
        k_rot = rope_apply(jnp.dot(normed, w_k, preferred_element_type=jnp.float32).reshape(tok_rows, n_kv, head_dim), cos_t, sin_t).astype(jnp.bfloat16)
        v_val = jnp.dot(normed, w_v, preferred_element_type=jnp.float32).astype(jnp.bfloat16).reshape(tok_rows, n_kv, head_dim)
        if repeat > 1:
            k_rot = jnp.repeat(k_rot, repeat, axis=1)
            v_val = jnp.repeat(v_val, repeat, axis=1)
        q_head = lax.all_to_all(q_rot, 'hp', 1, 0, tiled=True).reshape(pair_rows, loc_kv, loc_group, head_dim)
        k_head = lax.all_to_all(k_rot, 'hp', 1, 0, tiled=True)
        v_head = lax.all_to_all(v_val, 'hp', 1, 0, tiled=True)
        k_all = lax.all_gather(k_head, 'cp', axis=0, tiled=True)
        v_all = lax.all_gather(v_head, 'cp', axis=0, tiled=True)
        q_idx = pair_index(cp_idx, cp_size, pair_rows)
        k_idx = stored_index(cp_size, pair_rows)
        visible = q_idx[:, None] >= k_idx[None, :]
        scores = jnp.einsum('qkgd,tkd->kgqt', q_head, k_all, preferred_element_type=jnp.float32) * score_scale
        scores = jnp.where(visible, scores, -1e30)
        prob_f32 = jnp.exp(scores - jnp.max(scores, axis=-1, keepdims=True))
        prob_f32 = prob_f32 / jnp.sum(prob_f32, axis=-1, keepdims=True)
        prob_b16 = prob_f32.astype(jnp.bfloat16)
        out_head = jnp.einsum('kgqt,tkd->qkgd', prob_b16, v_all, preferred_element_type=jnp.float32).astype(jnp.bfloat16)
        attn_out = lax.all_to_all(out_head.reshape(pair_rows, loc_heads, head_dim), 'hp', 0, 1, tiled=True).reshape(tok_rows, n_heads * head_dim)
        output = (x_f32 + jnp.dot(attn_out, w_o, preferred_element_type=jnp.float32)).astype(jnp.bfloat16)
        grad_wo = jnp.einsum('ta,tb->ab', attn_out, grad_out, preferred_element_type=jnp.float32)
        d_out = jnp.einsum('tb,ab->ta', grad_out, w_o, preferred_element_type=jnp.float32).astype(jnp.bfloat16).reshape(tok_rows, n_heads, head_dim)
        do_head = lax.all_to_all(d_out, 'hp', 1, 0, tiled=True).reshape(pair_rows, loc_kv, loc_group, head_dim)
        row_delta = jnp.einsum('qkgd,qkgd->kgq', do_head, out_head, preferred_element_type=jnp.float32)
        d_prob = jnp.einsum('qkgd,tkd->kgqt', do_head, v_all, preferred_element_type=jnp.float32)
        d_score = (prob_f32 * (d_prob - row_delta[..., None])).astype(jnp.bfloat16)
        dq_head = (jnp.einsum('kgqt,tkd->qkgd', d_score, k_all, preferred_element_type=jnp.float32) * score_scale).astype(jnp.bfloat16)
        dk_part = (jnp.einsum('kgqt,qkgd->tkd', d_score, q_head, preferred_element_type=jnp.float32) * score_scale).astype(jnp.bfloat16)
        dv_part = jnp.einsum('kgqt,qkgd->tkd', prob_b16, do_head, preferred_element_type=jnp.float32).astype(jnp.bfloat16)
        dk_head = lax.psum_scatter(dk_part, 'cp', scatter_dimension=0, tiled=True)
        dv_head = lax.psum_scatter(dv_part, 'cp', scatter_dimension=0, tiled=True)
        dq_seq = lax.all_to_all(dq_head.reshape(pair_rows, loc_heads, head_dim), 'hp', 0, 1, tiled=True)
        dk_seq = lax.all_to_all(dk_head, 'hp', 0, 1, tiled=True)
        dv_seq = lax.all_to_all(dv_head, 'hp', 0, 1, tiled=True)
        if repeat > 1:
            dk_seq = jnp.sum(dk_seq.reshape(tok_rows, n_kv, repeat, head_dim).astype(jnp.float32), axis=2).astype(jnp.bfloat16)
            dv_seq = jnp.sum(dv_seq.reshape(tok_rows, n_kv, repeat, head_dim).astype(jnp.float32), axis=2).astype(jnp.bfloat16)
        g_q = rope_undo(dq_seq.astype(jnp.float32), cos_t, sin_t).astype(jnp.bfloat16).reshape(tok_rows, n_heads * head_dim)
        g_k = rope_undo(dk_seq.astype(jnp.float32), cos_t, sin_t).astype(jnp.bfloat16).reshape(tok_rows, n_kv * head_dim)
        g_v = dv_seq.reshape(tok_rows, n_kv * head_dim)
        grad_wq = jnp.einsum('ta,tb->ab', normed, g_q, preferred_element_type=jnp.float32)
        grad_wk = jnp.einsum('ta,tb->ab', normed, g_k, preferred_element_type=jnp.float32)
        grad_wv = jnp.einsum('ta,tb->ab', normed, g_v, preferred_element_type=jnp.float32)
        d_norm = jnp.einsum('tb,ab->ta', g_q, w_q, preferred_element_type=jnp.float32) + jnp.einsum('tb,ab->ta', g_k, w_k, preferred_element_type=jnp.float32) + jnp.einsum('tb,ab->ta', g_v, w_v, preferred_element_type=jnp.float32)
        grad_gain = jnp.sum(d_norm * x_hat, axis=0)
        d_hat = d_norm * norm_gain.astype(jnp.float32)
        grad_hidden = (grad_out.astype(jnp.float32) + inv_rms * (d_hat - x_hat * jnp.mean(d_hat * x_hat, axis=-1, keepdims=True))).astype(jnp.bfloat16)
        weight_grads = lax.psum((grad_wq, grad_wk, grad_wv, grad_wo, grad_gain), ('hp', 'cp'))
        return (output, grad_hidden) + tuple(weight_grads)

    seq_spec = P(('cp', 'hp'), None)
    whole = P()
    return jax.shard_map(device_step, mesh=mesh, in_specs=(seq_spec, seq_spec, P(('cp', 'hp')), whole, whole, whole, whole, whole, whole), out_specs=(seq_spec, seq_spec, whole, whole, whole, whole, whole), check_vma=False)
```

profile of v0, /device:TPU:0, one launch (start us, length us, event | category | flops | bytes accessed | tf_op | source)
XLA Modules:
  0.0 1831.8 jit_solution(4313073358707915799)
XLA Ops:
  7.8 1.4 fusion.39
  10.8 5.7 fusion.71
  17.4 6.4 all-to-all-start.1
  23.8 3.8 fusion.46
  28.4 4.1 all-to-all-done.1
  32.5 3.4 all-to-all-start
  36.8 12.7 fusion.45
  50.6 5.4 all-to-all-start.4
  56.0 7.8 convolution_bitcast_fusion.2
  66.8 8.6 all-to-all-done.4
  75.4 4.2 all-to-all-start.2
  79.7 2.3 broadcast_compare_fusion
  83.4 15.6 all-to-all-done.2
  100.2 25.4 %fusion.75 = (f32[2,3,512]{2,1,0:T(4,128)S(1)}, f32[2,3,512,4096]{2,3,1,0:T(8,128)}) fusion(pred[512,4096]{0,1:T(8,128)(4,1)} %broadcast_compare_fusion, bf16[512,2,3,128]{3,0,2,1:T(8,128)(2,1)S(1)} %bitcast.170, bf16[4096,2,128]{2,0,1:T(8,128)(2,1)} %all-gather.5.cloned.1.call-done), kind=kOutput, calls=%fused_computation.102 | convolution fusion | flops 3271561216 | bytes 55324672 | tf_op jit(solution)/shard_map/sub | solution.py:76
  125.6 26.1 %fusion.7 = bf16[2,3,512,4096]{2,3,1,0:T(8,128)(2,1)} fusion(f32[2,3,512,4096]{2,3,1,0:T(8,128)} %get-tuple-element.26, f32[2,3,512]{2,1,0:T(4,128)S(1)} %get-tuple-element.25), kind=kLoop, calls=%fused_computation.11 | loop fusion | flops 25165824 | bytes 75509760 | tf_op jit(solution)/shard_map/convert_element_type | solution.py:78
  151.7 14.5 fusion.11
  166.3 13.1 multiply_reduce_fusion
  179.4 38.3 %fusion.2 = bf16[2,3,512,4096]{2,3,1,0:T(8,128)(2,1)} fusion(f32[2,3,512]{2,1,0:T(4,128)S(1)} %get-tuple-element.27, f32[2,3,512,4096]{2,3,1,0:T(8,128)} %get-tuple-element.26, f32[2,3,512]{2,1,0:T(4,128)S(1)} %get-tuple-element.25, bf16[512,2,3,128]{3,0,2,1:T(8,128)(2,1)S(1)} %bitcast.165, bf16[4096,2,128]{0,2,1:T(8,128)(2,1)} %all-gather.3.cloned.1.call-done), kind=kOutput, calls=%fused_computation.3 | convolution fusion | flops 3271557120 | bytes 78405632 | tf_op jit(solution)/shard_map/qkgd,tkd->kgqt/dot_general | solution.py:86
  217.8 12.4 multiply_convert_fusion
  230.1 1.5 copy.150
  231.6 3.5 all-to-all-start.5
  235.2 14.0 fusion.14
  250.3 1.5 copy.142
  251.8 8.6 all-to-all-done.5
  261.3 3.5 all-to-all-start.3
  269.2 1.6 copy.153
  270.8 1.8 copy.160
  272.6 17.4 all-to-all-done.3
  290.0 3.4 all-to-all-start.7
  293.4 15.8 fusion.68
  309.2 1.7 copy.144
  311.0 1.8 copy.156
  312.8 5.0 all-to-all-start.6
  317.9 16.1 fusion.81
  335.8 2.0 copy.157
  338.9 6.7 fusion.64
  346.3 6.7 fusion.66
  353.0 14.0 fusion.80
  367.0 10.0 fusion.15
  377.0 5.2 convolution_add_fusion.1
  382.1 6.4 fusion.38
  388.5 41.7 %psum.39 = f32[3072]{0:T(1024)} all-reduce(f32[3072]{0:T(1024)S(1)} %get-tuple-element.7), channel_id=1, replica_groups=mesh['hp'=4,'cp'=8] {'hp','cp'}, use_global_device_ids=true, to_apply=%region_11.12 | all-reduce | flops 3072 | bytes 24576 | tf_op jit(solution)/shard_map/psum | solution.py:109
  430.2 2.8 fusion.37
  433.1 1312.1 %all-reduce.3.cloned.1.call-done = (f32[3072,3072]{1,0:T(8,128)}, f32[3072,1024]{1,0:T(8,128)}, f32[3072,1024]{1,0:T(8,128)}, f32[3072,3072]{1,0:T(8,128)}) async-done(((f32[3072,3072]{1,0:T(8,128)}, f32[3072,1024]{1,0:T(8,128)}, f32[3072,1024]{1,0:T(8,128)}, f32[3072,3072]{1,0:T(8,128)}), (f32[3072,3072]{1,0:T(8,128)}, f32[3072,1024]{1,0:T(8,128)}, f32[3072,1024]{1,0:T(8,128)}, ...) | async-done | bytes 100663312 | tf_op jit(solution)/shard_map/psum | solution.py:109
  1745.1 27.9 %copy.204 = f32[3072,3072]{1,0:T(8,128)} copy(f32[3072,3072]{1,0:T(8,128)} %get-tuple-element.32) | data formatting | bytes 75497472
  1773.0 12.1 copy.205
  1785.1 12.1 copy.206
  1797.2 27.9 %copy.207 = f32[3072,3072]{1,0:T(8,128)} copy(f32[3072,3072]{1,0:T(8,128)} %get-tuple-element.35) | data formatting | bytes 75497472
  (94 shorter events, 21.6 us)
Async XLA Ops:
  9.2 46.7 %copy-start.20 = (f32[128]{0:T(128)}, f32[128]{0:T(128)S(1)}, u32[]{:S(2)}) copy-start(f32[128]{0:T(128)S(1)} %add_rsqrt_fusion) | copy-start | bytes 1540
  9.9 46.1 %copy-start.10 = (f32[3072]{0:T(1024)}, f32[3072]{0:T(1024)S(1)}, u32[]{:S(2)}) copy-start(f32[3072]{0:T(1024)S(1)} %convert_element_type.95) | copy-start | bytes 36868
  10.8 53.0 %copy-start.16 = (f32[128,64]{0,1:T(8,128)}, f32[128,64]{0,1:T(8,128)S(1)}, u32[]{:S(2)}) copy-start(f32[128,64]{0,1:T(8,128)S(1)} %get-tuple-element.23) | copy-start | bytes 98308
  10.8 53.1 %copy-start.18 = (f32[128,64]{0,1:T(8,128)}, f32[128,64]{0,1:T(8,128)S(1)}, u32[]{:S(2)}) copy-start(f32[128,64]{0,1:T(8,128)S(1)} %get-tuple-element.24) | copy-start | bytes 98308
  16.5 7.4 copy-start
  17.4 15.1 all-to-all-start.1
  27.6 9.1 copy-start.2
  32.5 18.0 all-to-all-start
  35.9 64.3 %all-gather.5.cloned.1.call-start = ((), (), s32[]{:S(2)}) async-start(), calls=%async_computation.11 | async-start | bytes 2359296 | tf_op jit(solution)/shard_map/all_gather | solution.py:69
  50.6 24.8 %all-to-all-start.4 = ((bf16[128,24,128]{2,0,1:T(8,128)(2,1)}), bf16[128,24,128]{2,0,1:T(8,128)(2,1)S(1)}, u32[]{:S(2)}, u32[]{:S(2)}) async-start(bf16[128,24,128]{2,0,1:T(8,128)(2,1)} %bitcast.159), calls=%async_computation.4 | async-start | bytes 1572864 | tf_op jit(solution)/shard_map/all_to_all | solution.py:84
  63.9 0.9 copy-start.12
  64.0 0.8 copy-start.14
  75.4 23.6 %all-to-all-start.2 = ((bf16[128,24,128]{2,0,1:T(8,128)(2,1)}), bf16[128,24,128]{2,0,1:T(8,128)(2,1)}, u32[]{:S(2)}, u32[]{:S(2)}) async-start(bf16[128,24,128]{2,0,1:T(8,128)(2,1)} %pad_maximum_fusion), calls=%async_computation.2 | async-start | bytes 1572864 | tf_op jit(solution)/shard_map/all_to_all | solution.py:66
  79.6 86.7 %all-gather.3.cloned.1.call-start = ((), (), s32[]{:S(2)}) async-start(), calls=%async_computation.10 | async-start | bytes 2359296 | tf_op jit(solution)/shard_map/all_gather | solution.py:70
  83.0 187.8 %reduce-scatter.5.cloned.1.call-start = ((), (), s32[]{:S(2)}) async-start(), calls=%async_computation.13 | async-start | bytes 2359296 | tf_op jit(solution)/shard_map/reduce_scatter | solution.py:92
  231.6 28.7 %all-to-all-start.5 = ((bf16[512,6,128]{2,1,0:T(8,128)(2,1)}), bf16[512,6,128]{2,1,0:T(8,128)(2,1)S(1)}, u32[]{:S(2)}, u32[]{:S(2)}) async-start(bf16[512,6,128]{2,1,0:T(8,128)(2,1)} %copy.150), calls=%async_computation.5 | async-start | bytes 2097152 | tf_op jit(solution)/shard_map/all_to_all | solution.py:93
  235.1 75.8 %reduce-scatter.3.cloned.1.call-start = ((), (), s32[]{:S(2)}) async-start(), calls=%async_computation.12 | async-start | bytes 2359296 | tf_op jit(solution)/shard_map/reduce_scatter | solution.py:91
  249.2 1.1 copy-start.5
  260.3 1.0 copy-start.7
  261.3 28.7 %all-to-all-start.3 = ((bf16[512,6,128]{2,1,0:T(8,128)(2,1)}), bf16[512,6,128]{2,1,0:T(8,128)(2,1)S(1)}, u32[]{:S(2)}, u32[]{:S(2)}) async-start(bf16[512,6,128]{2,1,0:T(8,128)(2,1)} %copy.142), calls=%async_computation.3 | async-start | bytes 2097152 | tf_op jit(solution)/shard_map/all_to_all | solution.py:80
  266.3 0.8 copy-start.13
  266.3 0.9 copy-start.15
  269.2 24.2 %copy-start.1 = (bf16[128,3072]{1,0:T(8,128)(2,1)S(1)}, bf16[128,3072]{1,0:T(8,128)(2,1)}, u32[]{:S(2)}) copy-start(bf16[128,3072]{1,0:T(8,128)(2,1)} %param.9) | copy-start | bytes 2359300
  269.2 24.2 %copy-start.11 = (f32[3072]{0:T(1024)S(1)}, f32[3072]{0:T(1024)}, u32[]{:S(2)}) copy-start(f32[3072]{0:T(1024)} %copy-done.10) | copy-start | bytes 36868
  269.2 24.2 %copy-start.21 = (f32[128]{0:T(128)S(1)}, f32[128]{0:T(128)}, u32[]{:S(2)}) copy-start(f32[128]{0:T(128)} %copy-done.20) | copy-start | bytes 1540
  290.0 3.4 copy-start.6
  290.0 22.8 %all-to-all-start.7 = ((bf16[512,2,128]{2,1,0:T(2,128)(2,1)}), bf16[512,2,128]{2,1,0:T(2,128)(2,1)S(1)}, u32[]{:S(2)}, u32[]{:S(2)}) async-start(bf16[512,2,128]{2,1,0:T(2,128)(2,1)} %copy.160), calls=%async_computation.9 | async-start | bytes 524288 | tf_op jit(solution)/shard_map/all_to_all | solution.py:95
  309.2 8.6 copy-start.3
  312.8 23.0 %all-to-all-start.6 = ((bf16[512,2,128]{2,1,0:T(2,128)(2,1)}), bf16[512,2,128]{2,1,0:T(2,128)(2,1)}, u32[]{:S(2)}, u32[]{:S(2)}) async-start(bf16[512,2,128]{2,1,0:T(2,128)(2,1)} %copy.156), calls=%async_computation.7 | async-start | bytes 524288 | tf_op jit(solution)/shard_map/all_to_all | solution.py:94
  317.8 1427.3 %all-reduce.3.cloned.1.call-start = ((), (), s32[]{:S(2)}) async-start(), calls=%async_computation.14 | async-start | bytes 201326592 | tf_op jit(solution)/shard_map/psum | solution.py:109
  333.9 3.8 copy-start.17
  333.9 3.8 copy-start.19
  345.6 0.7 copy-start.8
  366.9 10.0 copy-start.4
  367.0 10.0 copy-start.9
Sparse Core Ops, SparseCore 0:
  39.2 28.9 all-gather.4
  83.1 29.1 all-gather.2
  166.4 40.1 reduce-scatter.4
  249.3 42.2 reduce-scatter.2
  353.1 1391.9 all-reduce.2
where the time goes:
time: 1840 us; the launch traced here: 1830 us
  waiting for transfers between devices  1370 us (74%)
  matrix products  229 us (12%)
  local copies, waits for them, and re-layouts  106 us (6%)
  blocking collectives  41.7 us (2%)
  other arithmetic  40.1 us (2%)
  starting transfers between devices  35 us (2%)
    psum x1, waiting for transfers between devices, device_step(): lax.psum((grad_wq, grad_wk, grad_wv, grad_wo, grad_gain), ('hp', 'cp'))  1310 us
    unnamed x50, local copies, waits for them, and re-layouts  84.2 us
    psum x1, blocking collectives, device_step(): lax.psum((grad_wq, grad_wk, grad_wv, grad_wo, grad_gain), ('hp', 'cp'))  41.7 us
    dot_general x1, matrix products, device_step(): jnp.einsum('qkgd,tkd->kgqt', do_head, v_all, preferred_element_type=jnp.f...  38.3 us
  transfers between devices with their start and end apart: 13, of which 6 were waited for; matrix products, arithmetic and copies ran while one was open for 14% of the time, Pallas kernels for 0%

commit v1 on v0

v1 whole, which is shorter than its diff:
```python
import functools
import jax
import jax.numpy as jnp
from jax import lax
from jax.experimental import pallas as pl
from jax.experimental.pallas import tpu as pltpu
from jax.sharding import PartitionSpec as P

NORM_EPS = 1e-5
F32 = jnp.float32
BF16 = jnp.bfloat16
LANES = 128
BLK = 512
HALF = BLK // 2
SEQ = 8 * BLK
QROWS = 2 * BLK
UPP = 8
LAG = 3
VMEM_LIMIT = 60 * 2**20
NT = (((1,), (1,)), ((), ()))
TN = (((0,), (0,)), ((), ()))

STAGES = {
    'C': ('z1', 'z2', 'z3', 'y', 'x', 'd'),
    'D': ('z1', 'z2', 'z3', 'x', 'y', 'd'),
    'E': ('x', 'y', 'z1', 'z2', 'z3', 'd'),
    'F': ('y', 'x', 'z1', 'z2', 'z3', 'd'),
}
SLOT = {'z1': 0, 'z2': 2, 'z3': 4, 'x': 6, 'y': 7, 'd': 8}
N_STAGE = 6
N_SLOT = 9


def rope_apply(vectors, cos_t, sin_t):
    half_dim = vectors.shape[-1] // 2
    lo_half = vectors[..., :half_dim]
    hi_half = vectors[..., half_dim:]
    return jnp.concatenate([lo_half * cos_t - hi_half * sin_t, hi_half * cos_t + lo_half * sin_t], axis=-1)


def rope_undo(vectors, cos_t, sin_t):
    half_dim = vectors.shape[-1] // 2
    lo_half = vectors[..., :half_dim]
    hi_half = vectors[..., half_dim:]
    return jnp.concatenate([lo_half * cos_t + hi_half * sin_t, hi_half * cos_t - lo_half * sin_t], axis=-1)


class Gather:
    def __init__(self, send_sem, recv_sem):
        self.z = lax.axis_index('hp')
        cp = lax.axis_index('cp')
        self.c, self.x, self.y = lax.rem(cp, 2), lax.rem(lax.div(cp, 2), 2), lax.div(cp, 4)
        self.send_sem, self.recv_sem = send_sem, recv_sem

    def device(self, c=None, x=None, y=None, z=None):
        c = self.c if c is None else c
        x = self.x if x is None else x
        y = self.y if y is None else y
        z = self.z if z is None else z
        return (z, y * 4 + x * 2 + c)

    def copies(self, sem_row, kind, view, stage):
        c, x, y, z = self.c, self.x, self.y, self.z
        order = STAGES[kind]
        done = {st[0] for st in order[:order.index(stage)]}
        every = slice(None)
        gx, gy, gz = (every if d in done else v for d, v in (('x', x), ('y', y), ('z', z)))
        slot = SLOT[stage]

        def copy(place, device, slot):
            return lambda: pltpu.make_async_remote_copy(
                place, place, self.send_sem.at[sem_row, slot], self.recv_sem.at[sem_row, slot],
                device_id=device, device_id_type=pl.DeviceIdType.MESH)

        if stage == 'x':
            dev = self.device(x=1 - x)
            return [(None, copy(view(c, x, gy, gz), dev, slot), None, copy(view(c, 1 - x, gy, gz), dev, slot))]
        if stage == 'y':
            dev = self.device(y=1 - y)
            return [(None, copy(view(c, gx, y, gz), dev, slot), None, copy(view(c, gx, 1 - y, gz), dev, slot))]
        if stage == 'd':
            dev = self.device(c=1 - c)
            return [(None, copy(view(c, every, every, every), dev, slot),
                     None, copy(view(1 - c, every, every, every), dev, slot))]
        hop = int(stage[1])
        up, down = self.device(z=jnp.minimum(z + 1, 3)), self.device(z=jnp.maximum(z - 1, 0))
        return [
            ((z >= hop - 1) & (z < 3), copy(view(c, gx, gy, jnp.maximum(z - hop + 1, 0)), up, slot),
             z >= hop, copy(view(c, gx, gy, jnp.maximum(z - hop, 0)), up, slot)),
            ((z + hop <= 4) & (z > 0), copy(view(c, gx, gy, jnp.minimum(z + hop - 1, 3)), down, slot + 1),
             z + hop <= 3, copy(view(c, gx, gy, jnp.minimum(z + hop, 3)), down, slot + 1)),
        ]

    def run(self, sem_row, kind, view, stage, what):
        for can_send, send, can_recv, recv in self.copies(sem_row, kind, view, stage):
            cond = can_recv if what == 'recv' else can_send

            def act(send=send, recv=recv):
                if what == 'start':
                    send().start()
                elif what == 'sent':
                    send().wait_send()
                else:
                    recv().wait_recv()

            if cond is None:
                act()
            else:
                pl.when(cond)(act)

    def advance(self, sem_row, kind, view, s):
        if s > 0:
            self.run(sem_row, kind, view, STAGES[kind][s - 1], 'recv')
        if s < N_STAGE:
            self.run(sem_row, kind, view, STAGES[kind][s], 'start')

    def kinds(self, u):
        w = lax.rem(u, 8)
        m = lax.rem(w, 3)
        return (('C', m == 0), ('D', m == 1), ('E', w == 2), ('F', w == 5))

    def tick(self, t, n_units, view):
        for s in range(N_STAGE + 1):
            u = t - s * LAG
            uc = jnp.clip(u, 0, n_units - 1)
            for kind, is_kind in self.kinds(uc):
                @pl.when((u >= 0) & (u < n_units) & is_kind)
                def _(kind=kind, s=s, uc=uc):
                    self.advance(uc, kind, view(uc), s)

    def drain(self, n_units, view):
        def body(u, carry):
            for kind, is_kind in self.kinds(u):
                @pl.when(is_kind)
                def _(kind=kind):
                    for stage in STAGES[kind]:
                        self.run(u, kind, view(u), stage, 'sent')
            return carry
        lax.fori_loop(0, n_units, body, 0)


def n_ticks(n_units):
    return n_units + N_STAGE * LAG


def turn(v):
    return pltpu.roll(v, LANES // 2, 1)


def cos_sin(cs):
    low = lax.broadcasted_iota(jnp.int32, cs.shape, 1) < LANES // 2
    other = turn(cs)
    return jnp.where(low, cs, other), jnp.where(low, -other, cs)


def gather_in_kernel(h_ref, dy_ref, cs_ref, wq_ref, wk_ref, wv_ref, wo_ref,
                     hd_ref, csg_ref, q_ref, k_ref, v_ref, do_ref,
                     rows_buf, cs_buf, wq_buf, wkv_buf, wo_buf, send_sem, recv_sem, csend, crecv, lsem, wsem, rsem, tsem):
    net = Gather(send_sem, recv_sem)
    small = Gather(csend, crecv)
    own = (net.y, net.x, net.c, net.z)
    head, quarter = net.c * 4 + net.z, net.y * 2 + net.x
    mine = [pltpu.make_async_copy(src, dst, lsem.at[i]) for i, (src, dst) in enumerate((
        (h_ref, hd_ref.at[(0, *own)]), (cs_ref, csg_ref.at[own]), (dy_ref, hd_ref.at[(1, *own)])))]
    for m in mine:
        m.start()
    q_cols = pl.ds(pl.multiple_of(head * 3 * LANES, LANES), 3 * LANES)
    kv_cols = pl.ds(pl.multiple_of(head * LANES, LANES), LANES)
    weights = [pltpu.make_async_copy(src, dst, wsem.at[i]) for i, (src, dst) in enumerate((
        (wq_ref.at[:, q_cols], wq_buf), (wk_ref.at[:, kv_cols], wkv_buf.at[:, :LANES]),
        (wv_ref.at[:, kv_cols], wkv_buf.at[:, LANES:]), (wo_ref.at[q_cols, :], wo_buf)))]
    for w in weights:
        w.start()
    for m in mine:
        m.wait()

    def view(u):
        rows = pl.ds(pl.multiple_of(lax.rem(u, 8) * 16, 16), 16)
        which = lax.div(u, 8)
        return lambda c, x, y, z: hd_ref.at[which, y, x, c, z, rows, :]

    def cs_view(c, x, y, z):
        return csg_ref.at[y, x, c, z]

    def blocks(which, pair):
        slot = lax.rem(pair, 2)
        y, x, c = lax.div(pair, 4), lax.rem(lax.div(pair, 2), 2), slot
        out = []
        for z in range(4):
            rows = pl.ds(z * LANES, LANES)
            out.append(pltpu.make_async_copy(hd_ref.at[which, y, x, c, z], rows_buf.at[slot, rows], rsem.at[slot, z]))
            if which == 0:
                out.append(pltpu.make_async_copy(csg_ref.at[y, x, c, z], cs_buf.at[slot, rows], tsem.at[slot, z]))
        return out

    def low(pair):
        return pl.ds(pl.multiple_of(pair * HALF, HALF), HALF)

    def to_queries(dst, value, side):
        for j in range(3):
            cols = slice(j * LANES, (j + 1) * LANES)
            dst[j, low(side), :] = value[:HALF, cols].astype(BF16)
            dst[j, low(3 - side), :] = value[HALF:, cols].astype(BF16)

    def project(pair):
        slot = lax.rem(pair, 2)
        for c in blocks(0, pair):
            c.wait()

        @pl.when(pair < 7)
        def _():
            for c in blocks(0, pair + 1):
                c.start()
        cos, sin = cos_sin(cs_buf[slot])
        kv = jnp.dot(rows_buf[slot], wkv_buf[...], preferred_element_type=F32)
        key = kv[:, :LANES]
        key = (key * cos + turn(key) * sin).astype(BF16)
        value = kv[:, LANES:].astype(BF16)
        for dst, src in ((k_ref, key), (v_ref, value)):
            dst[low(pair), :] = src[:HALF]
            dst[low(15 - pair), :] = src[HALF:]

        @pl.when(lax.div(pair, 2) == quarter)
        def _():
            q = jnp.dot(rows_buf[slot], wq_buf[...], preferred_element_type=F32)
            parts = [q[:, j * LANES:(j + 1) * LANES] for j in range(3)]
            to_queries(q_ref, jnp.concatenate([p * cos + turn(p) * sin for p in parts], axis=1), slot)

    ready = 8 + N_STAGE * LAG

    def body(t, carry):
        net.tick(t, 16, view)
        for s in range(N_STAGE + 1):
            @pl.when(t == 2 + s * LAG)
            def _(s=s):
                small.advance(0, 'D', cs_view, s)

        @pl.when(t == ready)
        def _():
            for c in blocks(0, jnp.int32(0)):
                c.start()
            for w in weights:
                w.wait()

        @pl.when((t > ready) & (t <= ready + 8))
        def _():
            project(t - ready - 1)
        return carry

    lax.fori_loop(0, ready + 9, body, 0)
    for side in range(2):
        for c in blocks(1, quarter * 2 + side):
            c.start()
    for side in range(2):
        for c in blocks(1, quarter * 2 + side):
            c.wait()
        to_queries(do_ref, lax.dot_general(rows_buf[side], wo_buf[...], NT, preferred_element_type=F32), side)
    net.drain(16, view)
    for stage in STAGES['D']:
        small.run(0, 'D', cs_view, stage, 'sent')


def any_spec():
    return pl.BlockSpec(memory_space=pl.ANY)


def vmem_spec():
    return pl.BlockSpec(memory_space=pltpu.VMEM)


def sems(*shape):
    return pltpu.SemaphoreType.DMA(shape)


def like(shape, dtype):
    return jax.ShapeDtypeStruct(shape, dtype)


def gather_in(h, dy, cs, w_q, w_k, w_v, w_o):
    model = h.shape[1]
    queries, keys = like((3, QROWS, LANES), BF16), like((SEQ, LANES), BF16)
    return pl.pallas_call(
        gather_in_kernel,
        out_shape=[like((2, 2, 2, 2, 4) + h.shape, BF16), like((2, 2, 2, 4) + cs.shape, F32), queries, keys, keys, queries],
        in_specs=[vmem_spec()] * 3 + [any_spec()] * 4,
        out_specs=[any_spec()] * 2 + [vmem_spec()] * 4,
        scratch_shapes=[pltpu.VMEM((2, BLK, model), BF16), pltpu.VMEM((2, BLK, LANES), F32),
                        pltpu.VMEM((model, 3 * LANES), BF16), pltpu.VMEM((model, 2 * LANES), BF16),
                        pltpu.VMEM((3 * LANES, model), BF16),
                        sems(16, N_SLOT), sems(16, N_SLOT), sems(1, N_SLOT), sems(1, N_SLOT),
                        sems(3), sems(4), sems(2, 4), sems(2, 4)],
        compiler_params=pltpu.CompilerParams(has_side_effects=True, vmem_limit_bytes=VMEM_LIMIT),
    )(h, dy, cs, w_q, w_k, w_v, w_o)


N_PIECE = 8
O_PIECE = 5
N_TILE = 6
PER_PIECE = 2 * N_TILE
IN_GATHER = 7
N_GATHER = IN_GATHER * PER_PIECE


def tile_product(operand, piece, of_output):
    left, right = (piece, operand) if of_output else (operand, piece)
    return lax.dot_general(left, right, TN, preferred_element_type=F32)


def operand_copy(hd_ref, abuf, asem, which, t, slot):
    return pltpu.make_async_copy(
        hd_ref.at[which, :, pl.ds(pl.multiple_of(t * BLK, BLK), BLK)], abuf.at[slot], asem.at[slot])


def piece_copies(g_ref, gbuf, gsem, p, core, slot):
    return [pltpu.make_async_copy(g_ref.at[p, core, z, r // 2, r % 2],
                                  gbuf.at[slot, pl.ds(r * QROWS, QROWS), pl.ds(z * LANES, LANES)], gsem.at[slot, z * 4 + r])
            for z in range(4) for r in range(4)]


def lane_groups(op, s):
    out = s[:, :LANES]
    for i in range(1, s.shape[1] // LANES):
        out = op(out, s[:, i * LANES:(i + 1) * LANES])
    return out


class Attention:
    def __init__(self, q, do, k, v, cs, out, dk_acc, dv_acc, s, state, quarter):
        self.q, self.do, self.k, self.v, self.cs, self.out = q, do, k, v, cs, out
        self.dk, self.dv, self.s, self.state = dk_acc, dv_acc, s, state
        self.quarter = quarter
        self.scale = LANES ** -0.5
        self.factor = self.scale * 1.4426950408889634

    def step(self, t):
        head, half = lax.div(t, 8), lax.rem(lax.div(t, 4), 2)
        n_key = jnp.where(half == 0, self.quarter + 1, SEQ // BLK - self.quarter)
        rows = pl.ds(pl.multiple_of(half * BLK, BLK), BLK)
        for i, act in enumerate((self.scores, self.exps, self.values, self.grads)):
            @pl.when(lax.rem(t, 4) == i)
            def _(act=act):
                act(head, half, n_key, rows)

    def keys(self, kb):
        return pl.ds(pl.multiple_of(kb * BLK, BLK), BLK)

    def zeros(self):
        return jnp.zeros((BLK, LANES), F32)

    def keep(self, i, column):
        self.state[i] = jnp.broadcast_to(column, (BLK, LANES))

    def kept(self, i):
        return self.state[i, :, :1]

    def scores(self, head, half, n_key, rows):
        q = self.q[head, rows, :]

        def block(kb, m, diagonal=False):
            s = lax.dot_general(q, self.k[self.keys(kb), :], NT, preferred_element_type=F32)
            if diagonal:
                visible = lax.broadcasted_iota(jnp.int32, s.shape, 0) >= lax.broadcasted_iota(jnp.int32, s.shape, 1)
                s = jnp.where(visible, s, -1e30)
            self.s[kb] = s
            return jnp.maximum(m, lane_groups(jnp.maximum, s))

        m = lax.fori_loop(0, n_key - 1, block, self.zeros() - 1e30)
        m = block(n_key - 1, m, diagonal=True)
        self.keep(0, jnp.max(m, axis=1, keepdims=True) * self.factor)

    def exps(self, head, half, n_key, rows):
        m = self.kept(0)

        def block(kb, total):
            e = jnp.exp2(self.s[kb] * self.factor - m)
            self.s[kb] = e
            return total + lane_groups(jnp.add, e)

        total = lax.fori_loop(0, n_key, block, self.zeros())
        self.keep(0, 1.0 / jnp.sum(total, axis=1, keepdims=True))

    def sides(self, half):
        for side in range(2):
            place = (half * (1 - side) + (1 - half) * side) * HALF
            yield pl.ds(pl.multiple_of(place, HALF), HALF), pl.ds(pl.multiple_of(side * BLK + half * HALF, HALF), HALF)

    def values(self, head, half, n_key, rows):
        do, inv = self.do[head, rows, :], self.kept(0)

        def block(kb, o):
            p = self.s[kb] * inv
            self.s[kb] = p
            p = p.astype(BF16)
            self.dv[self.keys(kb), :] += lax.dot_general(p, do, TN, preferred_element_type=F32)
            return o + jnp.dot(p, self.v[self.keys(kb), :], preferred_element_type=F32)

        o = lax.fori_loop(0, n_key, block, self.zeros()).astype(BF16).astype(F32)
        self.keep(0, jnp.sum(do.astype(F32) * o, axis=1, keepdims=True))
        self.state[1] = o
        for place, stored in self.sides(half):
            self.out[1, head, stored, :] = self.state[1, place, :].astype(BF16)

    def grads(self, head, half, n_key, rows):
        q, do, delta = self.q[head, rows, :], self.do[head, rows, :], self.kept(0)

        def block(kb, dq):
            dp = lax.dot_general(do, self.v[self.keys(kb), :], NT, preferred_element_type=F32)
            ds = (self.s[kb] * (dp - delta)).astype(BF16)
            self.dk[self.keys(kb), :] += lax.dot_general(ds, q, TN, preferred_element_type=F32)
            return dq + jnp.dot(ds, self.k[self.keys(kb), :], preferred_element_type=F32)

        dq = lax.fori_loop(0, n_key, block, self.zeros()) * self.scale
        self.state[1] = dq.astype(BF16).astype(F32)
        for place, stored in self.sides(half):
            cos, sin = cos_sin(self.cs[stored, :])
            part = self.state[1, place, :]
            self.out[0, head, stored, :] = (part * cos - turn(part) * sin).astype(BF16)

    def key_grads(self, out):
        for pair in range(8):
            for i, (acc, factor) in enumerate(((self.dk, self.scale), (self.dv, 1.0))):
                for part, block in enumerate((pair, 15 - pair)):
                    out[pair // 2, i, pl.ds(pair % 2 * BLK + part * HALF, HALF), :] = (
                        acc[pl.ds(block * HALF, HALF), :] * factor).astype(BF16)


N_STEP = 24
START = 8
N_UNIT = N_PIECE * UPP
GAIN_PARTS = 12
N_DEV = 32


def main_kernel(q_ref, do_ref, k_ref, v_ref, cs_ref, x_ref, dy_ref, gain_ref, hd_ref, wq_ref, wk_ref, wv_ref,
                g_ref, t_ref, o_ref, dx_ref, dgain_ref,
                piece_buf, dk_acc, dv_acc, s_buf, state, dkv_buf, peer_buf, gbuf, abuf, obuf, own_buf, w_buf, dn_buf, part_buf, parts,
                send_sem, recv_sem, lsem, gsem, asem, osem, tsend, trecv, psend, precv, rsem, wsem, gain_send, gain_recv):
    net = Gather(send_sem, recv_sem)
    quarter = net.y * 2 + net.x
    model = x_ref.shape[1]
    attn = Attention(q_ref, do_ref, k_ref, v_ref, cs_ref, piece_buf, dk_acc, dv_acc, s_buf, state, quarter)
    dk_acc[...] = jnp.zeros_like(dk_acc)
    dv_acc[...] = jnp.zeros_like(dv_acc)

    def local(p, src):
        return pltpu.make_async_copy(src, g_ref.at[p, net.c, net.z, net.y, net.x], lsem.at[p])

    def head_pieces(head):
        return [local(head + p, piece_buf.at[i, head]) for i, p in ((0, 0), (1, O_PIECE))]

    peers = []
    for i, (dx, dy) in enumerate(((1, 0), (0, 1), (1, 1))):
        x, y = (1 - net.x if dx else net.x), (1 - net.y if dy else net.y)
        peers.append(functools.partial(
            pltpu.make_async_remote_copy, dkv_buf.at[y * 2 + x], peer_buf.at[i], psend.at[i], precv.at[i],
            device_id=net.device(x=x, y=y), device_id_type=pl.DeviceIdType.MESH))

    def add_peers():
        for peer in peers:
            peer().wait_recv()
        total = dkv_buf[quarter].astype(F32)
        for i in range(3):
            total = total + peer_buf[i].astype(F32)
        total = total.astype(BF16)
        cos, sin = cos_sin(cs_ref[...])
        dk = total[0].astype(F32)
        piece_buf[0, 0] = (dk * cos - turn(dk) * sin).astype(BF16)
        piece_buf[0, 1] = total[1]
        kv = [local(3 + i, piece_buf.at[0, i]) for i in range(2)]
        for copy in kv:
            copy.start()
        for copy in kv:
            copy.wait()

    def view(u):
        unit_rows = QROWS // UPP
        rows = pl.ds(pl.multiple_of(lax.rem(u, UPP) * unit_rows, unit_rows), unit_rows)
        p = lax.div(u, UPP)
        return lambda c, x, y, z: g_ref.at[p, c, z, y, x, rows, :]

    def place(n):
        return lax.div(n, N_TILE) * PER_PIECE + lax.rem(n, N_TILE) * 2 + net.c

    def keep_tile(n, slot):
        return pltpu.make_async_copy(obuf.at[slot], t_ref.at[place(n)], osem.at[slot])

    def give_tile(n, slot):
        return pltpu.make_async_remote_copy(
            obuf.at[slot], t_ref.at[place(n)], tsend.at[slot], trecv.at[n],
            device_id=net.device(c=1 - net.c), device_id_type=pl.DeviceIdType.MESH)

    def operand(n):
        return operand_copy(hd_ref, abuf, asem, jnp.where(n < O_PIECE * N_TILE, 0, 1), lax.rem(n, N_TILE), lax.rem(n, 2))

    def piece(p):
        return piece_copies(g_ref, gbuf, gsem, p, net.c, lax.rem(p, 2))

    n_own = IN_GATHER * N_TILE

    def tile(n, carry):
        slot = lax.rem(n, 3)
        p = lax.div(n, N_TILE)

        @pl.when(lax.rem(n, N_TILE) == 0)
        def _():
            for copy in piece(p):
                copy.wait()
        operand(n).wait()

        @pl.when(n + 1 < n_own)
        def _():
            operand(n + 1).start()

        @pl.when(n >= 3)
        def _():
            keep_tile(n, slot).wait()
            give_tile(n, slot).wait_send()
        for of_output in (False, True):
            @pl.when((p >= O_PIECE) == of_output)
            def _(of_output=of_output):
                obuf[slot] = tile_product(abuf[lax.rem(n, 2)], gbuf[lax.rem(p, 2)], of_output)
        keep_tile(n, slot).start()
        give_tile(n, slot).start()
        return carry

    def own_copies(p):
        rows = pl.ds(pl.multiple_of(net.c * BLK + net.z * LANES, LANES), LANES)
        for g in range(8):
            if p < 3:
                dst, col = own_buf, 3 * g + p
            elif p < O_PIECE:
                dst, col = own_buf, 8 * p + g
            else:
                dst, col = o_ref, 3 * g + p - O_PIECE
            yield pltpu.make_async_copy(
                g_ref.at[p, g // 4, g % 4, net.y, net.x, rows, :], dst.at[:, pl.ds(col * LANES, LANES)], rsem.at[p, g])

    def own(pieces, wait):
        for p in pieces:
            for copy in own_copies(p):
                if wait:
                    copy.wait()
                else:
                    copy.start()

    def weight_rows(i):
        slot = lax.rem(i, 2)
        rows = pl.ds(pl.multiple_of(i * HALF, HALF), HALF)
        kv = wk_ref.shape[1]
        return [pltpu.make_async_copy(src.at[rows, :], w_buf.at[slot, :, cols], wsem.at[slot, j]) for j, (src, cols) in enumerate((
            (wq_ref, slice(0, 3 * kv)), (wk_ref, slice(3 * kv, 4 * kv)), (wv_ref, slice(4 * kv, 5 * kv))))]

    def inv_rms():
        x = x_ref[...].astype(F32)
        return lax.rsqrt(jnp.mean(x * x, axis=-1, keepdims=True) + NORM_EPS)

    def norm_grad(i):
        slot = lax.rem(i, 2)
        for copy in weight_rows(i):
            copy.wait()

        @pl.when(i + 1 < GAIN_PARTS)
        def _():
            for copy in weight_rows(i + 1):
                copy.start()
        cols = pl.ds(pl.multiple_of(i * HALF, HALF), HALF)
        dn = lax.dot_general(own_buf[...], w_buf[slot], NT, preferred_element_type=F32)
        dn_buf[:, cols] = dn
        x_hat = x_ref[:, cols].astype(F32) * inv_rms()
        part = jnp.sum(dn * x_hat, axis=0, keepdims=True)
        for j in range(2):
            part_buf[pl.ds(i * 2 + j, 1), :] = part[:, j * LANES:(j + 1) * LANES]

    me = lax.axis_index('cp') * 4 + net.z

    def gain_copy(step, slot):
        other = lax.rem(me + step, N_DEV)
        return pltpu.make_async_remote_copy(
            part_buf, parts.at[slot], gain_send.at[step], gain_recv.at[slot],
            device_id=(lax.rem(other, 4), lax.div(other, 4)), device_id_type=pl.DeviceIdType.MESH)

    def others(act):
        def run(step, carry):
            act(step)
            return carry
        lax.fori_loop(1, N_DEV, run, 0)

    def input_grad():
        x_hat = x_ref[...].astype(F32) * inv_rms()
        d_hat = dn_buf[...] * gain_ref[...].astype(F32)
        dx_ref[...] = (dy_ref[...].astype(F32) + inv_rms() * (
            d_hat - x_hat * jnp.mean(d_hat * x_hat, axis=-1, keepdims=True))).astype(BF16)

    operand(jnp.int32(0)).start()
    kv_tick = START + 3 * UPP
    own_tick = START + O_PIECE * UPP + N_STAGE * LAG

    def body(t, carry):
        n, loaded = carry

        @pl.when((t > 0) & (t <= N_STEP) & (lax.rem(t, 8) == 0))
        def _():
            for copy in head_pieces(lax.div(t, 8) - 1):
                copy.wait()

        @pl.when(t == N_STEP)
        def _():
            attn.key_grads(dkv_buf)
            for peer in peers:
                peer().start()

        @pl.when(t == kv_tick)
        def _():
            add_peers()
        net.tick(t - START, N_UNIT, view)

        @pl.when(t < N_STEP)
        def _():
            attn.step(t)

            @pl.when(lax.rem(t, 8) == 7)
            def _():
                for copy in head_pieces(lax.div(t, 8)):
                    copy.start()

        complete = jnp.minimum(lax.div(jnp.maximum(t - START - (N_STAGE - 1) * LAG + 1, 0), UPP), IN_GATHER)
        load = (loaded < complete) & (loaded <= lax.div(n, N_TILE) + 1)

        @pl.when(load)
        def _():
            for copy in piece(loaded):
                copy.start()

        @pl.when(t == own_tick)
        def _():
            own(range(O_PIECE), False)
            for copy in weight_rows(jnp.int32(0)):
                copy.start()

        @pl.when(t == own_tick + 1)
        def _():
            own(range(O_PIECE), True)

        @pl.when((t > own_tick) & (t <= own_tick + GAIN_PARTS))
        def _():
            norm_grad(t - own_tick - 1)

        @pl.when(t == own_tick + GAIN_PARTS + 1)
        def _():
            mine = pltpu.make_async_copy(part_buf, parts.at[me], gain_send.at[0])
            mine.start()
            mine.wait()
            others(lambda step: gain_copy(step, me).start())
            input_grad()

        n_end = jnp.minimum(jnp.minimum(n + 1, loaded * N_TILE), n_own)
        lax.fori_loop(n, n_end, tile, 0)
        return n_end, loaded + load.astype(jnp.int32)

    n, _ = lax.fori_loop(0, START + n_ticks(N_UNIT) + 1, body, (jnp.int32(0), jnp.int32(0)))
    own(range(O_PIECE, N_PIECE), False)
    lax.fori_loop(n, n_own, tile, 0)
    others(lambda step: gain_copy(step, lax.rem(me + step, N_DEV)).wait_recv())
    dgain_ref[...] = jnp.sum(parts[...], axis=0)
    for slot in range(3):
        keep_tile(0, slot).wait()
        give_tile(0, slot).wait_send()

    def received(n, carry):
        give_tile(n, 0).wait_recv()
        return carry

    lax.fori_loop(0, n_own, received, 0)
    own(range(O_PIECE, N_PIECE), True)
    for peer in peers:
        peer().wait_send()
    others(lambda step: gain_copy(step, me).wait_send())
    net.drain(N_UNIT, view)


def main(q, do, k, v, cs, x, dy, gain, hd, w_q, w_k, w_v):
    model = x.shape[1]
    qkv = w_q.shape[1] + w_k.shape[1] + w_v.shape[1]
    return pl.pallas_call(
        main_kernel,
        out_shape=[like((N_PIECE, 2, 4, 2, 2, QROWS, LANES), BF16), like((N_GATHER, BLK, BLK), F32),
                   like((LANES, model), BF16), like(x.shape, BF16), like((2 * GAIN_PARTS, LANES), F32)],
        in_specs=[vmem_spec()] * 8 + [any_spec()] * 4,
        out_specs=[any_spec()] * 2 + [vmem_spec()] * 3,
        scratch_shapes=[
            pltpu.VMEM((2, 3, QROWS, LANES), BF16), pltpu.VMEM((SEQ, LANES), F32), pltpu.VMEM((SEQ, LANES), F32),
            pltpu.VMEM((SEQ // BLK, BLK, BLK), F32), pltpu.VMEM((2, BLK, LANES), F32),
            pltpu.VMEM((4, 2, QROWS, LANES), BF16), pltpu.VMEM((3, 2, QROWS, LANES), BF16),
            pltpu.VMEM((2, SEQ, BLK), BF16), pltpu.VMEM((2, SEQ, BLK), BF16), pltpu.VMEM((3, BLK, BLK), F32),
            pltpu.VMEM((LANES, qkv), BF16), pltpu.VMEM((2, HALF, qkv), BF16), pltpu.VMEM(x.shape, F32),
            pltpu.VMEM((2 * GAIN_PARTS, LANES), F32), pltpu.VMEM((N_DEV, 2 * GAIN_PARTS, LANES), F32),
            sems(N_UNIT, N_SLOT), sems(N_UNIT, N_SLOT), sems(N_PIECE), sems(2, 16), sems(2), sems(3), sems(3),
            sems(IN_GATHER * N_TILE), sems(3), sems(3), sems(N_PIECE, 8), sems(2, 3), sems(N_DEV), sems(N_DEV)],
        compiler_params=pltpu.CompilerParams(has_side_effects=True, vmem_limit_bytes=VMEM_LIMIT),
    )(q, do, k, v, cs, x, dy, gain, hd, w_q, w_k, w_v)


GROUP = IN_GATHER


def finish_kernel(hd_ref, g_ref, t_ref, wq_ref, wk_ref, wv_ref, wo_ref,
                  gbuf, abuf, obuf, cbuf, gsem, asem, osem, isem, csem):
    n_step, group = PER_PIECE, GROUP

    def operand(t):
        return operand_copy(hd_ref, abuf, asem, 1, t, lax.rem(t, 2))

    def cut(t):
        return pl.ds(pl.multiple_of(t * BLK, BLK), BLK)

    def lanes(i):
        return pl.ds(pl.multiple_of(i * LANES, LANES), LANES)

    def to_output(p, t, sub, src, sem):
        return [pltpu.make_async_copy(
            src.at[pl.ds(i * LANES, LANES), :], wo_ref.at[lanes(3 * (sub * 4 + i) + p - O_PIECE), cut(t)], sem.at[i])
            for i in range(4)]

    def to_input(dst, place, t, sub, src, sem):
        return [pltpu.make_async_copy(
            src.at[:, pl.ds(i * LANES, LANES)], dst.at[cut(t), lanes(place(sub * 4 + i))], sem.at[i]) for i in range(4)]

    def ins(n):
        return [pltpu.make_async_copy(t_ref.at[n * group + i], cbuf.at[lax.rem(n, 3), i], isem.at[lax.rem(n, 3), i])
                for i in range(group)]

    def start_outs(n):
        for i in range(group):
            m = n * group + i
            p, t, sub = lax.div(m, PER_PIECE), lax.rem(lax.div(m, 2), N_TILE), lax.rem(m, 2)
            src, sem = cbuf.at[lax.rem(n, 3), i], csem.at[lax.rem(n, 3), i]
            for cond, copies in (
                (p < 3, lambda: to_input(wq_ref, lambda g: 3 * g + p, t, sub, src, sem)),
                (p == 3, lambda: to_input(wk_ref, lambda g: g, t, sub, src, sem)),
                (p == 4, lambda: to_input(wv_ref, lambda g: g, t, sub, src, sem)),
                (p >= O_PIECE, lambda: to_output(p, t, sub, src, sem)),
            ):
                @pl.when(cond)
                def _(copies=copies):
                    for c in copies():
                        c.start()

    def wait_outs(n):
        for i in range(group):
            for c in to_output(O_PIECE, 0, 0, cbuf.at[0, i], csem.at[lax.rem(n, 3), i]):
                c.wait()

    for sub in range(2):
        for c in piece_copies(g_ref, gbuf, gsem, IN_GATHER, sub, sub):
            c.start()
    operand(jnp.int32(0)).start()

    def step(n, carry):
        t, p, sub = lax.div(n, 2), IN_GATHER, lax.rem(n, 2)
        slot = lax.rem(n, 3)

        @pl.when(n >= 3)
        def _():
            wait_outs(n - 3)
        for c in ins(n):
            c.start()

        @pl.when(n >= 1)
        def _():
            for c in ins(n - 1):
                c.wait()
            start_outs(n - 1)

        @pl.when(sub == 0)
        def _():
            operand(t).wait()

            @pl.when(t + 1 < N_TILE)
            def _():
                operand(t + 1).start()

        @pl.when(n < 2)
        def _():
            for c in piece_copies(g_ref, gbuf, gsem, p, sub, sub):
                c.wait()

        @pl.when(n >= 3)
        def _():
            for c in to_output(O_PIECE, 0, 0, obuf.at[0], osem.at[slot]):
                c.wait()
        obuf[slot] = tile_product(abuf[lax.rem(t, 2)], gbuf[sub], True)
        for c in to_output(p, t, sub, obuf.at[slot], osem.at[slot]):
            c.start()
        return carry

    lax.fori_loop(0, n_step, step, 0)
    for c in ins(n_step - 1):
        c.wait()
    start_outs(jnp.int32(n_step - 1))
    for n in range(n_step - 3, n_step):
        wait_outs(n)
        for c in to_output(O_PIECE, 0, 0, obuf.at[0], osem.at[n % 3]):
            c.wait()


def finish(hd, g, tiles):
    model, kv = hd.shape[2], 8 * LANES
    return pl.pallas_call(
        finish_kernel,
        out_shape=[like((model, n), F32) for n in (3 * kv, kv, kv)] + [like((3 * kv, model), F32)],
        in_specs=[any_spec()] * 3,
        out_specs=[any_spec()] * 4,
        scratch_shapes=[pltpu.VMEM((2, SEQ, BLK), BF16), pltpu.VMEM((2, SEQ, BLK), BF16), pltpu.VMEM((3, BLK, BLK), F32),
                        pltpu.VMEM((3, GROUP, BLK, BLK), F32),
                        sems(2, 16), sems(2), sems(3, 4), sems(3, GROUP), sems(3, GROUP, 4)],
        cost_estimate=pl.CostEstimate(flops=2 * SEQ * kv * model, bytes_accessed=250 * 2**20, transcendentals=0),
        compiler_params=pltpu.CompilerParams(vmem_limit_bytes=VMEM_LIMIT),
    )(hd, g, tiles)


def solution(mesh):
    assert mesh.shape['hp'] == 4 and mesh.shape['cp'] == 8

    def device_step(hidden, grad_out, positions, norm_gain, w_q, w_k, w_v, w_o, inv_freq):
        model = hidden.shape[1]
        quarter = lax.div(lax.axis_index('cp'), 2)
        gain = norm_gain.astype(F32)
        x_f32 = hidden.astype(F32)
        inv_rms = lax.rsqrt(jnp.mean(x_f32 * x_f32, axis=-1, keepdims=True) + NORM_EPS)
        x_hat = x_f32 * inv_rms
        normed = (x_hat * gain).astype(BF16)
        angles = positions.astype(F32)[:, None] * inv_freq[None, :]
        cs = jnp.concatenate([jnp.cos(angles), jnp.sin(angles)], axis=1)

        hd, csg, q, k, v, d_out = gather_in(normed, grad_out, cs, w_q, w_k, w_v, w_o)
        hd = hd.reshape(2, SEQ, model)
        cs_rows = lax.dynamic_slice(csg.reshape(SEQ, LANES), (quarter * QROWS, 0), (QROWS, LANES))
        gathered, tiles, o_own, grad_hidden, gains = main(
            q, d_out, k, v, cs_rows, hidden, grad_out, norm_gain.reshape(1, model), hd, w_q, w_k, w_v)
        grad_wq, grad_wk, grad_wv, grad_wo = finish(hd, gathered, tiles)
        output = (x_f32 + jnp.dot(o_own, w_o, preferred_element_type=F32)).astype(BF16)
        grad_gain = gains.reshape(-1)
        return output, grad_hidden, grad_wq, grad_wk, grad_wv, grad_wo, grad_gain

    rows, whole = P(('cp', 'hp'), None), P()
    return jax.shard_map(
        device_step, mesh=mesh,
        in_specs=(rows, rows, P(('cp', 'hp')), whole, whole, whole, whole, whole, whole),
        out_specs=(rows, rows, whole, whole, whole, whole, whole), check_vma=False)
```

time: 1840 us -> 683 us (0.37)
  waiting for transfers between devices: 1370 us -> 0 us
  Pallas kernels: 0 us -> 660 us
  matrix products: 229 us -> 10.1 us
  local copies, waits for them, and re-layouts: 106 us -> 4.67 us
  blocking collectives: 41.7 us -> 0 us
  starting transfers between devices: 35 us -> 0 us
  other arithmetic: 40.1 us -> 6.68 us
    psum x1 -> x0, waiting for transfers between devices: 1310 us -> none  [device_step(): lax.psum((grad_wq, grad_wk, grad_wv, grad_wo, grad_gain), ('hp', 'cp'))]
    pallas_call x0 -> x3, Pallas kernels: none -> 660 us  [the longest x1 345 us: main(): pl.pallas_call(main_kernel, out_shape=[like((N_PIECE, 2, 4, 2, 2, QROWS,...]
    dot_general x16 -> x1, matrix products: 198 us -> 10.1 us  [device_step(): jnp.dot(o_own, w_o, preferred_element_type=F32)]
    unnamed x50 -> x8, local copies, waits for them, and re-layouts: 84.2 us -> 1.49 us
    all_to_all x8 -> x0, waiting for transfers between devices: 54.2 us -> none  [the longest x1 17.4 us: device_step(): lax.all_to_all(out_head.reshape(pair_rows, loc_heads, head_dim), 'hp', 0,...]
    psum x1 -> x0, blocking collectives: 41.7 us -> none  [device_step(): lax.psum((grad_wq, grad_wk, grad_wv, grad_wo, grad_gain), ('hp', 'cp'))]
    all_to_all x8 -> x0, starting transfers between devices: 34.9 us -> none  [the longest x1 6.38 us: device_step(): k_head = lax.all_to_all(k_rot, 'hp', 1, 0, tiled=True)]
    convert_element_type x5 -> x3, other arithmetic: 30.4 us -> 3.63 us  [the longest x1 2.27 us: device_step(): normed = (x_hat * gain).astype(BF16)]
  transfers between devices with their start and end apart: 13 -> 0, of which waited for: 6 -> 0; matrix products, arithmetic and copies ran while one was open for 14% -> 0% of each run, Pallas kernels for 0% -> 0%
where the time goes in v1:
time: 683 us; the launch traced here: 682 us
  Pallas kernels  660 us (97%)
  matrix products  10.1 us (1%)
    pallas_call x1, Pallas kernels, main(): pl.pallas_call(main_kernel, out_shape=[like((N_PIECE, 2, 4, 2, 2, QROWS,...  345 us
    pallas_call x1, Pallas kernels, gather_in(): pl.pallas_call(gather_in_kernel, out_shape=[like((2, 2, 2, 2, 4) + h.shap...  242 us
    pallas_call x1, Pallas kernels, finish(): pl.pallas_call(finish_kernel, out_shape=[like((model, n), F32) for n in (...  72.5 us

profile of v1, /device:TPU:0, one launch (start us, length us, event | category | flops | bytes accessed | tf_op | source)
XLA Modules:
  0.0 681.7 jit_solution(1945438082831482233)
XLA Ops:
  0.6 0.7 convert_element_type.18
  1.3 1.4 fusion.1
  2.7 1.3 reshape.38.gain_ref
  4.0 0.7 convert_element_type.16
  4.7 1.0 multiply_cosine_fusion
  5.6 0.7 pad_maximum_fusion.cs_ref
  6.4 2.3 fusion.3.h_ref
  8.6 241.5 %shard_map.144 = (bf16[2,2,2,2,4,128,3072]{6,5,4,3,2,1,0:T(8,128)(2,1)}, f32[2,2,2,4,128,128]{5,4,3,2,1,0:T(8,128)}, bf16[3,1024,128]{2,1,0:T(8,128)(2,1)}, bf16...) custom-call(bf16[128,3072]{1,0:T(8,128)(2,1)} %fusion.3.h_ref, ...), custom_call_target="tpu_custom_call" | custom-call | tf_op jit(solution)/shard_map/pallas_call | solution.py:282
  250.2 1.9 constant_dynamic-slice_fusion.cs_ref
  252.1 0.0 copy-start
  252.1 345.5 %shard_map.145 = (bf16[8,2,4,2,2,1024,128]{6,5,4,3,2,1,0:T(8,128)(2,1)}, f32[84,512,512]{2,1,0:T(8,128)}, bf16[128,3072]{1,0:T(8,128)(2,1)}, bf16[128,3072]{1,0:T(8,128)(2,1)}, f32[24,128]{1,0:T(8,128)}) custom-call(bf16[3,1024,128]{2,1,0:T(8,128)(2,1)} %get-tuple-element.22.q_ref, bf16[3,1024,128]{2,1,0:T(8,128)(2,1)} %get-tuple-element.23.do_ref, ...), custom_call_target="tpu_custom_call" | custom-call | tf_op jit(solution)/shard_map/pallas_call | solution.py:684
  597.5 0.0 copy-done
  597.5 10.1 %fusion = bf16[128,3072]{1,0:T(8,128)(2,1)} fusion(bf16[128,3072]{1,0:T(8,128)(2,1)} %get-tuple-element.28, bf16[3072,3072]{1,0:T(8,128)(2,1)} %wo_ref.1, bf16[128,3072]{1,0:T(8,128)(2,1)S(1)} %copy-done), kind=kOutput, calls=%fused_computation.1 | convolution fusion | flops 2417098752 | bytes 21233664 | tf_op jit(solution)/shard_map/dot_general | solution.py:841
  607.7 0.0 copy-start.1
  607.7 0.0 copy-start.2
  607.7 72.5 %shard_map.146 = (f32[3072,3072]{1,0:T(8,128)}, f32[3072,1024]{1,0:T(8,128)}, f32[3072,1024]{1,0:T(8,128)}, f32[3072,3072]{1,0:T(8,128)}) custom-call(bf16[2,4096,3072]{2,1,0:T(8,128)(2,1)} %bitcast.6, bf16[8,2,4,2,2,1024,128]{6,5,4,3,2,1,0:T(8,128)(2,1)} %get-tuple-element.30.g_ref, f32[84,512,512]{2,1,0:T(8,128)} %get-tuple-element.31.t_ref), custom_call_target="tpu_custom_call" | custom-call | flops 25769803776 | bytes 262144000 | tf_op jit(solution)/shard_map/pallas_call | solution.py:808
  680.2 0.0 copy-done.1
  680.2 0.9 copy.18
  681.1 0.0 copy-done.2
  681.1 0.6 copy.19
  (1 shorter events, 0.0 us)
Async XLA Ops:
  252.1 345.5 %copy-start = (bf16[128,3072]{1,0:T(8,128)(2,1)S(1)}, bf16[128,3072]{1,0:T(8,128)(2,1)}, u32[]{:S(2)}) copy-start(bf16[128,3072]{1,0:T(8,128)(2,1)} %x_ref.1) | copy-start | bytes 2359300
  607.7 72.5 %copy-start.1 = (bf16[128,3072]{1,0:T(8,128)(2,1)S(1)}, bf16[128,3072]{1,0:T(8,128)(2,1)}, u32[]{:S(2)}) copy-start(bf16[128,3072]{1,0:T(8,128)(2,1)} %get-tuple-element.47) | copy-start | bytes 2359300
  607.7 73.4 %copy-start.2 = (f32[24,128]{1,0:T(8,128)S(1)}, f32[24,128]{1,0:T(8,128)}, u32[]{:S(2)}) copy-start(f32[24,128]{1,0:T(8,128)} %get-tuple-element.36) | copy-start | bytes 36868

commit v2 on v0

v2 whole, which is shorter than its diff:
```python
import functools
import jax
import jax.numpy as jnp
from jax import lax
from jax.experimental import pallas as pl
from jax.experimental.pallas import tpu as pltpu
from jax.sharding import PartitionSpec as P

NORM_EPS = 1e-5
ALL = Ellipsis
EVERY = slice(None)
PAIR, TRIO, QUAD = 2, 3, 4
GRID = (PAIR, PAIR, PAIR, QUAD)
BY_COLUMN = {'axis': 0, 'keepdims': True}
BY_ROW = {'axis': 1, 'keepdims': True}
F32 = jnp.float32
BF16 = jnp.bfloat16
LANES = 128
BLK = 512
HALF = BLK // 2
SEQ = 8 * BLK
QROWS = PAIR * BLK
UPP = 8
LAG = 2
RING = 20
VMEM_LIMIT = 64 * 2**20 - 2**16
NT = (((1,), (1,)), ((), ()))
TN = (((0,), (0,)), ((), ()))

STAGES = {
    'C': ('z1', 'z2', 'z3', 'y', 'x', 'd'),
    'D': ('z1', 'z2', 'z3', 'x', 'y', 'd'),
    'E': ('x', 'y', 'z1', 'z2', 'z3', 'd'),
    'F': ('y', 'x', 'z1', 'z2', 'z3', 'd'),
}
SLOT = {'z1': 0, 'z2': 2, 'z3': 4, 'x': 6, 'y': 7, 'd': 8}
N_STAGE = 6
N_SLOT = 9


def odd(i):
    return lax.rem(i, PAIR)


def half_of(i):
    return lax.div(i, PAIR)


def nxt(i):
    return i + 1


def zero():
    return jnp.int32(0)


def loop(n, body, init):
    return lax.fori_loop(0, n, body, init)


class Gather:
    def __init__(self, send_sem, recv_sem, period, base=0):
        self.period, self.base = period, base
        self.z = lax.axis_index('hp')
        cp = lax.axis_index('cp')
        self.c, self.x, self.y = odd(cp), odd(half_of(cp)), lax.div(cp, 4)
        self.send_sem, self.recv_sem = send_sem, recv_sem

    def device(self, **moved):
        at = {name: moved.get(name, getattr(self, name)) for name in 'cxyz'}
        return at['z'], (at['y'] * PAIR + at['x']) * PAIR + at['c']

    def copies(self, sem_row, kind, view, stage):
        c, x, y, z = self.c, self.x, self.y, self.z
        order = STAGES[kind]
        done = {st[0] for st in order[:order.index(stage)]}
        every = EVERY
        gx, gy, gz = (every if d in done else v for d, v in (('x', x), ('y', y), ('z', z)))
        slot = SLOT[stage]

        def copy(place, device, slot):
            return lambda: pltpu.make_async_remote_copy(
                place, place, self.send_sem.at[sem_row, slot], self.recv_sem.at[sem_row, slot],
                device_id=device, device_id_type=pl.DeviceIdType.MESH)

        if stage == 'x':
            dev = self.device(x=1 - x)
            return [(None, copy(view(c, x, gy, gz), dev, slot), None, copy(view(c, 1 - x, gy, gz), dev, slot))]
        if stage == 'y':
            dev = self.device(y=1 - y)
            return [(None, copy(view(c, gx, y, gz), dev, slot), None, copy(view(c, gx, 1 - y, gz), dev, slot))]
        if stage == 'd':
            dev = self.device(c=1 - c)
            return [(None, copy(view(c, every, every, every), dev, slot),
                     None, copy(view(1 - c, every, every, every), dev, slot))]
        hop = int(stage[1])
        up, down = self.device(z=jnp.minimum(z + 1, 3)), self.device(z=jnp.maximum(z - 1, 0))
        return [
            ((z >= hop - 1) & (z < 3), copy(view(c, gx, gy, jnp.maximum(z - hop + 1, 0)), up, slot),
             z >= hop, copy(view(c, gx, gy, jnp.maximum(z - hop, 0)), up, slot)),
            ((z + hop <= 4) & (z > 0), copy(view(c, gx, gy, jnp.minimum(z + hop - 1, 3)), down, slot + 1),
             z + hop <= 3, copy(view(c, gx, gy, jnp.minimum(z + hop, 3)), down, slot + 1)),
        ]

    def run(self, sem_row, kind, view, stage, what):
        for can_send, send, can_recv, recv in self.copies(sem_row, kind, view, stage):
            cond = can_recv if what == 'recv' else can_send

            def act(send=send, recv=recv):
                if what == 'start':
                    send().start()
                elif what == 'sent':
                    send().wait_send()
                else:
                    recv().wait_recv()

            if cond is None:
                act()
            else:
                pl.when(cond)(act)

    def advance(self, sem_row, kind, view, s):
        if 0 < s <= N_STAGE:
            self.run(sem_row, kind, view, STAGES[kind][s - 1], 'recv')
        if s < N_STAGE:
            self.run(sem_row, kind, view, STAGES[kind][s], 'start')
        if s > N_STAGE:
            for stage in STAGES[kind]:
                self.run(sem_row, kind, view, stage, 'sent')

    def kinds(self, u):
        w, even = lax.rem(u, self.period), odd(u) == 0
        e, f = w == 0, w == self.period - 5
        return (('C', ~(e | f) & even), ('D', ~(e | f) & ~even), ('E', e), ('F', f))

    def tick(self, t, n_units, view):
        for s in range(N_STAGE + 2):
            u = t - s * LAG

            @pl.when((u >= 0) & (u < n_units))
            def _(u=u, s=s):
                for kind, is_kind in self.kinds(u):
                    @pl.when(is_kind)
                    def _(kind=kind):
                        self.advance(lax.rem(u + self.base, RING), kind, view(u), s)


def turn(v):
    return pltpu.roll(v, LANES // 2, 1)


def low_lanes(shape):
    return lax.broadcasted_iota(jnp.int32, shape, 1) < LANES // 2


def cos_sin(cs):
    low = low_lanes(cs.shape)
    other = turn(cs)
    return jnp.where(low, cs, other), jnp.where(low, -other, cs)


def any_spec():
    return pl.BlockSpec(memory_space=pl.ANY)


def vmem_spec():
    return pl.BlockSpec(memory_space=pltpu.VMEM)


def sems(*shape):
    return pltpu.SemaphoreType.DMA(shape) if shape else pltpu.SemaphoreType.DMA


def like(shape, dtype):
    return jax.ShapeDtypeStruct(shape, dtype)


def start_all(copies):
    for copy in copies:
        copy.start()


def wait_all(copies):
    for copy in copies:
        copy.wait()


N_PIECE = 8
O_PIECES = (3, 6, 7)
KEY_PIECE = 4
N_TILE = 6
PER_PIECE = PAIR * N_TILE
IN_GATHER = 7
N_GATHER = IN_GATHER * PER_PIECE


def tile_product(operand, piece, of_output):
    left, right = (piece, operand) if of_output else (operand, piece)
    return lax.dot_general(left, right, TN, preferred_element_type=F32)


def operand_copy(hd_ref, abuf, asem, which, t, slot):
    return pltpu.make_async_copy(
        hd_ref.at[which, :, pl.ds(pl.multiple_of(t * BLK, BLK), BLK)], abuf.at[slot], asem.at[slot])


def piece_copies(g_ref, gbuf, gsem, p, core, slot):
    return [pltpu.make_async_copy(g_ref.at[p, core, z, r // 2, r % 2],
                                  gbuf.at[slot, pl.ds(r * QROWS, QROWS), pl.ds(z * LANES, LANES)], gsem.at[slot])
            for z in range(QUAD) for r in range(QUAD)]


def wait_piece(gbuf, gsem, slot):
    pltpu.make_async_copy(gbuf.at[slot], gbuf.at[slot], gsem.at[slot]).wait()


def lane_groups(op, s):
    out = s[:, :LANES]
    for i in range(1, s.shape[1] // LANES):
        out = op(out, s[:, i * LANES:(i + 1) * LANES])
    return out


class Attention:
    def __init__(self, q, do, k, v, cs, out, dk_acc, dv_acc, s, state, quarter):
        self.q, self.do, self.k, self.v, self.cs, self.out = q, do, k, v, cs, out
        self.dk, self.dv, self.s, self.state = dk_acc, dv_acc, s, state
        self.quarter = quarter
        self.scale = LANES ** -0.5
        self.factor = self.scale * 1.4426950408889634

    def step(self, t):
        head, half = lax.div(t, 8), odd(lax.div(t, 4))
        n_key = jnp.where(half == 0, self.quarter + 1, SEQ // BLK - self.quarter)
        rows = pl.ds(pl.multiple_of(half * BLK, BLK), BLK)
        for i, act in enumerate((self.scores, self.exps, self.values, self.grads)):
            @pl.when(lax.rem(t, 4) == i)
            def _(act=act):
                act(head, half, n_key, rows)

    def keys(self, kb):
        return pl.ds(pl.multiple_of(kb * BLK, BLK), BLK)

    def zeros(self):
        return jnp.zeros((BLK, LANES), F32)

    def keep(self, i, column):
        self.state[i] = jnp.broadcast_to(column, (BLK, LANES))

    def kept(self, i):
        return self.state[i, :, :1]

    def scores(self, head, half, n_key, rows):
        q = self.q[head, rows, :]

        def block(kb, m, diagonal=False):
            s = lax.dot_general(q, self.k[self.keys(kb), :], NT, preferred_element_type=F32)
            if diagonal:
                visible = lax.broadcasted_iota(jnp.int32, s.shape, 0) >= lax.broadcasted_iota(jnp.int32, s.shape, 1)
                s = jnp.where(visible, s, -1e30)
            self.s[kb] = s
            return jnp.maximum(m, lane_groups(jnp.maximum, s))

        m = loop(n_key - 1, block, self.zeros() - 1e30)
        m = block(n_key - 1, m, diagonal=True)
        self.keep(0, jnp.max(m, **BY_ROW) * self.factor)

    def exps(self, head, half, n_key, rows):
        m = self.kept(0)

        def block(kb, total):
            e = jnp.exp2(self.s[kb] * self.factor - m)
            self.s[kb] = e
            return total + lane_groups(jnp.add, e)

        total = loop(n_key, block, self.zeros())
        self.keep(0, 1.0 / jnp.sum(total, **BY_ROW))

    def sides(self, half):
        for side in range(PAIR):
            place = (half * (1 - side) + (1 - half) * side) * HALF
            yield pl.ds(pl.multiple_of(place, HALF), HALF), pl.ds(pl.multiple_of(side * BLK + half * HALF, HALF), HALF)

    def values(self, head, half, n_key, rows):
        do, inv = self.do[head, rows, :], self.kept(0)
        turned = do.T

        def block(kb, o):
            p = (self.s[kb] * inv).astype(BF16)
            self.dv[:, self.keys(kb)] += jnp.dot(turned, p, preferred_element_type=F32)
            return o + jnp.dot(p, self.v[self.keys(kb), :], preferred_element_type=F32)

        o = loop(n_key, block, self.zeros()).astype(BF16).astype(F32)
        self.keep(1, jnp.sum(do.astype(F32) * o, **BY_ROW))
        self.state[2] = o
        for place, stored in self.sides(half):
            self.out[1, head, stored, :] = self.state[2, place, :].astype(BF16)

    def grads(self, head, half, n_key, rows):
        do, inv, delta = self.do[head, rows, :], self.kept(0), self.kept(1)
        turned = self.q[head, rows, :].T

        def block(kb, dq):
            dp = lax.dot_general(do, self.v[self.keys(kb), :], NT, preferred_element_type=F32)
            ds = (self.s[kb] * inv * (dp - delta)).astype(BF16)
            self.dk[:, self.keys(kb)] += jnp.dot(turned, ds, preferred_element_type=F32)
            return dq + jnp.dot(ds, self.k[self.keys(kb), :], preferred_element_type=F32)

        dq = loop(n_key, block, self.zeros()) * self.scale
        self.state[2] = dq.astype(BF16).astype(F32)
        for place, stored in self.sides(half):
            cos, sin = cos_sin(self.cs[stored, :])
            part = self.state[2, place, :]
            self.out[0, head, stored, :] = (part * cos - turn(part) * sin).astype(BF16)

    def key_grads(self, out):
        for pair in range(8):
            for i, (acc, factor) in enumerate(((self.dk, self.scale), (self.dv, 1.0))):
                for part, block in enumerate((pair, 15 - pair)):
                    out[pair // 2, i, pl.ds(pair % PAIR * BLK + part * HALF, HALF), :] = (
                        acc[:, pl.ds(block * HALF, HALF)].T * factor).astype(BF16)


ROWS_UNIT = 8
N_IN = LANES // ROWS_UNIT
N_STEP = 24
N_UNIT = N_PIECE * UPP
N_PART = 12
SEND_DO = N_PART + 1
DELAY = N_STAGE * LAG
CHUNK = PAIR * ROWS_UNIT
N_CHUNK = LANES // CHUNK
PROJECT = DELAY + 2
ATTEND = PROJECT + PAIR * N_CHUNK - 1
ATTENDED = ATTEND + N_STEP
START = ATTEND + 4
N_SEND = 8
KEYS_IN = START + KEY_PIECE * UPP
QUERY_IN = START + 3 * UPP + DELAY
OWN_IN = START + O_PIECES[1] * UPP + DELAY
OUT_IN = OWN_IN + N_PART // 2 + 2
N_OUT = 8
LAST = START + N_UNIT + DELAY + LAG
N_DEV = 32


def main_kernel(x_ref, dy_ref, gain_ref, mypos_ref, freq_ref, wq_ref, wk_ref, wv_ref, wo_ref,
                hd_ref, pos_ref, g_ref, t_ref, o_ref, sum_ref, dx_ref, dgain_ref,
                h_buf, q_buf, do_buf, k_buf, v_buf, rows_buf, mypos_buf, gain_buf, freq_buf, pos_buf, pos_t, cs_buf, own_cs, do_parts,
                piece_buf, dk_acc, dv_acc, s_buf, state, dkv_buf, peer_buf, gbuf, abuf, obuf, own_buf, oo_buf, w_buf, dn_buf, part_buf, parts,
                cs_send, cs_recv, send_sem, recv_sem, first_sem, proj_sem, rows_sem, do_send, do_recv,
                lsem, gsem, asem, osem, tsend, trecv, psend, precv, rsem, wsem, gain_send, gain_recv):
    net_in, net_cs, net = Gather(send_sem, recv_sem, 9), Gather(cs_send, cs_recv, 9), Gather(send_sem, recv_sem, 8, START)
    quarter = net.y * 2 + net.x
    head = net.c * 4 + net.z
    spot = (net.y, net.x, net.c, net.z)
    attn = Attention(q_buf, do_buf, k_buf, v_buf, own_cs, piece_buf, dk_acc, dv_acc, s_buf, state, quarter)

    def inv_rms():
        x = x_ref[ALL].astype(F32)
        return lax.rsqrt(jnp.mean(x * x, **BY_ROW) + NORM_EPS)

    me = lax.axis_index('cp') * 4 + net.z

    def device_at(step):
        other = lax.rem(me + step, N_DEV)
        return lax.rem(other, 4), lax.div(other, 4)

    barrier = pltpu.get_barrier_semaphore()

    def greet(step, carry):
        pl.semaphore_signal(barrier, inc=1, device_id=device_at(step), device_id_type=pl.DeviceIdType.MESH)
        return carry

    lax.fori_loop(1, N_DEV, greet, 0)

    gain_buf[ALL] = gain_ref[ALL].astype(F32).reshape(gain_buf.shape)
    freq_buf[ALL] = jnp.concatenate([freq_ref[ALL], freq_ref[ALL]], axis=0).reshape(freq_buf.shape)
    mypos_buf[ALL] = jnp.broadcast_to(mypos_ref[ALL].astype(F32).reshape(1, LANES), mypos_buf.shape)
    h_buf[ALL] = (x_ref[ALL].astype(F32) * inv_rms() * gain_buf[ALL]).astype(BF16)
    first = [pltpu.make_async_copy(src, dst, first_sem.at[i]) for i, (src, dst) in enumerate((
        (h_buf, hd_ref.at[(0, *spot)]), (dy_ref, hd_ref.at[(1, *spot)]), (mypos_buf, pos_ref.at[spot])))]
    start_all(first)
    wait_all(first)
    pl.semaphore_wait(barrier, N_DEV - 1)
    q_cols = pl.ds(pl.multiple_of(head * TRIO * LANES, LANES), TRIO * LANES)
    kv_cols = pl.ds(pl.multiple_of(head * LANES, LANES), LANES)
    w_rows = slice(0, wq_ref.shape[0])
    wq_buf, wkv_buf = gbuf.at[0, w_rows, :TRIO * LANES], gbuf.at[1, w_rows, :PAIR * LANES]
    weights = [pltpu.make_async_copy(src, dst, proj_sem.at[i]) for i, (src, dst) in enumerate((
        (wq_ref.at[:, q_cols], wq_buf), (wk_ref.at[:, kv_cols], gbuf.at[1, w_rows, :LANES]),
        (wv_ref.at[:, kv_cols], gbuf.at[1, w_rows, LANES:PAIR * LANES])))]

    def view_in(u):
        rows = pl.ds(pl.multiple_of(lax.rem(u, N_IN) * ROWS_UNIT, ROWS_UNIT), ROWS_UNIT)
        which = lax.div(u, N_IN)
        return lambda c, x, y, z: hd_ref.at[which, y, x, c, z, rows, :]

    def view_cs(c, x, y, z):
        return pos_ref.at[y, x, c, z]

    def part(i, width=HALF):
        return pl.ds(pl.multiple_of(i * width, width), width)

    def wo_rows(i):
        slot = odd(i)
        return pltpu.make_async_copy(wo_ref.at[part(i), :], w_buf.at[slot, :, :wo_ref.shape[1]], wsem.at[slot, 0])

    def head_grad(i):
        slot = odd(i)
        wo_rows(i).wait()

        @pl.when(nxt(i) < N_PART)
        def _():
            wo_rows(nxt(i)).start()
        own_buf[:, part(i)] = lax.dot_general(
            dy_ref[ALL], w_buf[slot, :, :wo_ref.shape[1]], NT, preferred_element_type=F32).astype(BF16)

    def do_copy(step, mine):
        me = net.c * 4 + net.z
        other = lax.rem(me + step, 8)
        slot = me if mine else lax.rem(me + 8 - step, 8)
        return pltpu.make_async_remote_copy(
            own_buf.at[:, part(other, TRIO * LANES)], do_parts.at[slot], do_send.at[step], do_recv.at[step],
            device_id=net.device(c=lax.div(other, 4), z=lax.rem(other, 4)), device_id_type=pl.DeviceIdType.MESH)

    own_do = pltpu.make_async_copy(own_buf.at[:, part(head, TRIO * LANES)], do_parts.at[head], do_send.at[0])

    def query_row(c, z):
        return c * HALF + z * LANES if z < 2 else BLK + (1 - c) * HALF + (z - 2) * LANES

    def take_do():
        for step in range(1, 8):
            do_copy(step, False).wait_recv()
        for c in range(PAIR):
            for z in range(QUAD):
                for j in range(TRIO):
                    do_buf[j, pl.ds(query_row(c, z), LANES), :] = do_parts[c * 4 + z, :, j * LANES:(j + 1) * LANES]

    every = EVERY

    def chunk(k, base=0):
        return pl.ds(pl.multiple_of(base + k * CHUNK, CHUNK), CHUNK)

    def chunk_rows(k):
        return pltpu.make_async_copy(hd_ref.at[0, every, every, every, every, chunk(k), every], rows_buf, rows_sem)

    def take_positions():
        copy = pltpu.make_async_copy(pos_ref, pos_buf, rows_sem)
        copy.start()
        copy.wait()
        for i in range(PAIR):
            pos_t[i] = pos_buf[i].reshape(LANES, LANES).T

    def angles(k):
        for dev in range(N_DEV):
            column = pos_t[dev // 16, chunk(k), dev % 16 * 8:dev % 16 * 8 + 1]
            cs_buf[dev * CHUNK:(dev + 1) * CHUNK, :] = jnp.broadcast_to(column, (CHUNK, LANES)) * freq_buf[ALL]
        angle = cs_buf[ALL]
        cs_buf[ALL] = jnp.where(low_lanes(angle.shape), jnp.cos(angle), jnp.sin(angle))

    def rotate(v, cs):
        cos, sin = cos_sin(cs)
        return (v * cos + turn(v) * sin).astype(BF16)

    def project(k):
        chunk_rows(k).wait()
        n_rows = N_DEV * CHUNK
        kv = jnp.dot(rows_buf[ALL].reshape(n_rows, -1), wkv_buf[ALL], preferred_element_type=F32)
        key = rotate(kv[:, :LANES], cs_buf[ALL])
        value = kv[:, LANES:].astype(BF16)
        for cp in range(8):
            for z in range(QUAD):
                block = 2 * cp + z if z < 2 else 28 - 2 * cp + z
                rows = slice((cp * 4 + z) * CHUNK, (cp * 4 + z + 1) * CHUNK)
                k_buf[chunk(k, block * LANES), :] = key[rows]
                v_buf[chunk(k, block * LANES), :] = value[rows]
        mine, cs = rows_buf[net.y, net.x].reshape(LANES, -1), cs_buf[part(quarter, LANES), :]
        q = jnp.dot(mine, wq_buf[ALL], preferred_element_type=F32)
        for j in range(TRIO):
            p = rotate(q[:, j * LANES:(j + 1) * LANES], cs)
            for c in range(PAIR):
                for z in range(QUAD):
                    rows = slice((c * 4 + z) * CHUNK, (c * 4 + z + 1) * CHUNK)
                    q_buf[j, chunk(k, query_row(c, z)), :] = p[rows]
                    if j == 0:
                        own_cs[chunk(k, c * BLK + z * LANES), :] = cs[rows]

    def local(p, i, src, rows=pl.ds(0, QROWS)):
        return pltpu.make_async_copy(src, g_ref.at[p, net.c, net.z, net.y, net.x, rows, :], lsem.at[p, i])

    def step_pieces(step):
        head, half = lax.div(step, 8), odd(lax.div(step, 4))
        out_piece = jnp.where(head == 0, O_PIECES[0], O_PIECES[0] + 2 + head)
        return [local(p, side, piece_buf.at[i, head, rows], rows) for i, p in ((0, head), (1, out_piece))
                for side, (_, rows) in enumerate(attn.sides(half))]

    def key_copies(rows):
        for i, moved in enumerate(('x', 'y', 'xy')):
            x, y = (1 - at if name in moved else at for name, at in (('x', net.x), ('y', net.y)))
            yield pltpu.make_async_remote_copy(
                dkv_buf.at[y * 2 + x, :, rows], peer_buf.at[i, :, rows], psend.at[i], precv.at[i],
                device_id=net.device(x=x, y=y), device_id_type=pl.DeviceIdType.MESH)

    def add_peers():
        for copy in key_copies(pl.ds(0, QROWS)):
            copy.wait_recv()
        total = dkv_buf[quarter].astype(F32)
        for i in range(TRIO):
            total = total + peer_buf[i].astype(F32)
        total = total.astype(BF16)
        cos, sin = cos_sin(own_cs[ALL])
        dk = total[0].astype(F32)
        piece_buf[0, 0] = (dk * cos - turn(dk) * sin).astype(BF16)
        piece_buf[0, 1] = total[1]
        kv = [local(KEY_PIECE + i, 0, piece_buf.at[0, i]) for i in range(PAIR)]
        start_all(kv)
        wait_all(kv)

    def view(u):
        p, k = lax.div(u, UPP), lax.rem(u, UPP)
        two = half_of(k)
        rows = part(odd(two) * 4 + half_of(two) * 2 + odd(k), QROWS // UPP)
        return lambda c, x, y, z: g_ref.at[p, c, z, y, x, rows, :]

    def place(n):
        return lax.div(n, N_TILE) * PER_PIECE + lax.rem(n, N_TILE) * 2 + net.c

    def keep_tile(n, slot):
        return pltpu.make_async_copy(obuf.at[slot], t_ref.at[place(n)], osem.at[slot])

    def give_tile(n, slot):
        return pltpu.make_async_remote_copy(
            obuf.at[slot], t_ref.at[place(n)], tsend.at[slot], trecv.at[n],
            device_id=net.device(c=1 - net.c), device_id_type=pl.DeviceIdType.MESH)

    def of_output(p):
        return (p == O_PIECES[0]) | (p == O_PIECES[1])

    def operand(n):
        which, slot = of_output(lax.div(n, N_TILE)).astype(jnp.int32), odd(n)
        return pltpu.make_async_copy(
            hd_ref.at[which, every, every, every, every, every, part(lax.rem(n, N_TILE), BLK)], abuf.at[slot], asem.at[slot])

    def piece(p):
        return piece_copies(g_ref, gbuf, gsem, p, net.c, odd(p))

    n_own = IN_GATHER * N_TILE

    def tile(n, carry):
        slot = lax.rem(n, TRIO)
        p = lax.div(n, N_TILE)

        @pl.when(lax.rem(n, N_TILE) == 0)
        def _():
            wait_piece(gbuf, gsem, odd(p))
        operand(n).wait()

        @pl.when(nxt(n) < n_own)
        def _():
            operand(nxt(n)).start()

        @pl.when(n >= 3)
        def _():
            keep_tile(n, slot).wait()
            give_tile(n, slot).wait_send()
        for output in (False, True):
            @pl.when(of_output(p) == output)
            def _(output=output):
                obuf[slot] = tile_product(abuf[odd(n)].reshape(SEQ, BLK), gbuf[odd(p)], output)
        keep_tile(n, slot).start()
        give_tile(n, slot).start()
        return carry

    kv = wk_ref.shape[1]
    groups = (((0, 1, 2), own_buf, slice(0, TRIO * kv)), ((KEY_PIECE, KEY_PIECE + 1), own_buf, slice(TRIO * kv, 5 * kv)),
              (O_PIECES[:2], oo_buf, slice(0, PAIR * kv)), (O_PIECES[2:], o_ref, slice(0, kv)))

    def start_own(i):
        rows = pl.ds(pl.multiple_of(net.c * BLK + net.z * LANES, LANES), LANES)
        pieces, dst, cols = groups[i]
        for k, p in enumerate(pieces):
            for g in range(8):
                col = cols.start // LANES + (TRIO * g + k if len(pieces) == 3 else 8 * k + g)
                pltpu.make_async_copy(
                    g_ref.at[p, g // 4, g % 4, net.y, net.x, rows, :], dst.at[:, pl.ds(col * LANES, LANES)], rsem.at[i]).start()

    def wait_own(i):
        _, dst, cols = groups[i]
        pltpu.make_async_copy(dst.at[:, cols], dst.at[:, cols], rsem.at[i]).wait()

    def weight_rows(turn, i):
        slot = odd(i)
        if turn == 0:
            places = ((wq_ref, part(i), 0, TRIO * kv),)
        else:
            places = [(src, part(i * 2 + j), (j * 2 + k) * kv, kv) for j in range(PAIR) for k, src in enumerate((wk_ref, wv_ref))]
        return [pltpu.make_async_copy(src.at[rows, :], w_buf.at[slot, :, pl.ds(at, width)], wsem.at[slot, j])
                for j, (src, rows, at, width) in enumerate(places)]

    def norm_grad(turn, i, n_steps):
        slot = odd(i)
        wait_all(weight_rows(turn, i))

        @pl.when(nxt(i) < n_steps)
        def _():
            start_all(weight_rows(turn, nxt(i)))
        if turn == 0:
            dn_buf[:, part(i)] = lax.dot_general(
                own_buf[:, :TRIO * kv], w_buf[slot, :, :TRIO * kv], NT, preferred_element_type=F32)
            return
        for j in range(PAIR):
            block = i * 2 + j
            dn = dn_buf[:, part(block)] + lax.dot_general(
                own_buf[:, TRIO * kv:], w_buf[slot, :, pl.ds(j * PAIR * kv, PAIR * kv)], NT, preferred_element_type=F32)
            dn_buf[:, part(block)] = dn
            x_hat = x_ref[:, part(block)].astype(F32) * inv_rms()
            total = jnp.sum(dn * x_hat, **BY_COLUMN)
            for k in range(PAIR):
                part_buf[pl.ds(block * 2 + k, 1), :] = total[:, k * LANES:(k + 1) * LANES]

    def send_gain(step, carry):
        pltpu.make_async_remote_copy(
            part_buf, parts.at[me], gain_send, gain_recv,
            device_id=device_at(step), device_id_type=pl.DeviceIdType.MESH).start()
        return carry

    def all_gains():
        rest = parts.at[pl.ds(1, N_DEV - 1)]
        return pltpu.make_async_remote_copy(
            rest, rest, gain_send, gain_recv, device_id=net.device(c=1 - net.c), device_id_type=pl.DeviceIdType.MESH)

    def input_grad():
        x_hat = x_ref[ALL].astype(F32) * inv_rms()
        d_hat = dn_buf[ALL] * gain_buf[ALL]
        dx_ref[ALL] = (dy_ref[ALL].astype(F32) + inv_rms() * (
            d_hat - x_hat * jnp.mean(d_hat * x_hat, **BY_ROW))).astype(BF16)

    n_cols = x_ref.shape[1] // BLK

    def out_rows(i):
        slot = odd(i)
        head = lax.rem(i, 4) * 6 + lax.div(i, 4)
        return [pltpu.make_async_copy(
            wo_ref.at[part(head + TRIO * j, LANES), :], w_buf.at[slot, j * LANES:(j + 1) * LANES, :wo_ref.shape[1]], wsem.at[slot, j])
            for j in range(PAIR)]

    def out_part(i):
        slot = odd(i)
        wait_all(out_rows(i))

        @pl.when(nxt(i) < N_OUT)
        def _():
            start_all(out_rows(nxt(i)))
        left = oo_buf[:, part(i)]
        for j in range(n_cols):
            cols = slice(j * BLK, (j + 1) * BLK)
            term = jnp.dot(left, w_buf[slot, :, cols], preferred_element_type=F32)
            before = jnp.where(i == 0, x_ref[:, cols].astype(F32), s_buf[j, :LANES, :])
            s_buf[j, :LANES, :] = before + term

    def body(t, carry):
        n, loaded = carry
        since = t - ATTEND

        @pl.when(t == 1)
        def _():
            wo_rows(zero()).start()
            start_all(weights)

        @pl.when(t == SEND_DO + 1)
        def _():
            own_do.start()
            for step in range(1, 8):
                do_copy(step, True).start()
            wait_all(weights)

        @pl.when((since > 0) & (t <= ATTENDED) & (lax.rem(since, 4) == 0))
        def _():
            wait_all(step_pieces(since - 1))

        @pl.when(t == ATTENDED)
        def _():
            attn.key_grads(dkv_buf)

        @pl.when((t >= ATTENDED) & (t < ATTENDED + N_SEND))
        def _():
            start_all(key_copies(part(t - ATTENDED, QROWS // N_SEND)))

        @pl.when(t == KEYS_IN)
        def _():
            add_peers()
        net_in.tick(t, PAIR * N_IN, view_in)
        net.tick(t - START, N_UNIT, view)
        for s in range(N_STAGE + 2):
            @pl.when(t == s * LAG)
            def _(s=s):
                net_cs.advance(0, 'D', view_cs, s)

        @pl.when((t > 1) & (t <= N_PART + 1))
        def _():
            head_grad(t - 2)

        ahead = t - PROJECT + 1

        @pl.when(ahead == 0)
        def _():
            take_positions()
            angles(0)

        @pl.when((ahead >= 0) & (odd(ahead) == 0) & (ahead < PAIR * N_CHUNK))
        def _():
            chunk_rows(half_of(ahead)).start()

        @pl.when((ahead > 0) & (odd(ahead) == 1) & (ahead < PAIR * N_CHUNK))
        def _():
            project(half_of(ahead))

            @pl.when(half_of(ahead) + 1 < N_CHUNK)
            def _():
                angles(half_of(ahead) + 1)

        @pl.when(t == ATTEND)
        def _():
            own_do.wait()
            take_do()
            operand(zero()).start()
            dk_acc[ALL] = jnp.zeros_like(dk_acc)
            dv_acc[ALL] = jnp.zeros_like(dv_acc)

        @pl.when((t >= ATTEND) & (t < ATTENDED))
        def _():
            attn.step(since)

            @pl.when(lax.rem(since, 4) == 3)
            def _():
                start_all(step_pieces(since))

        complete = jnp.minimum(lax.div(jnp.maximum(t - START - (N_STAGE - 1) * LAG + 1, 0), UPP), IN_GATHER)
        load = (loaded < complete) & (loaded <= lax.div(n, N_TILE) + 1)

        @pl.when(load)
        def _():
            start_all(piece(loaded))

        @pl.when(t == QUERY_IN)
        def _():
            for step in range(1, 8):
                do_copy(step, True).wait_send()

        for turn, (tick, n_steps) in enumerate(((QUERY_IN, N_PART), (OWN_IN, N_PART // 2))):
            @pl.when(t == tick)
            def _(turn=turn):
                start_own(turn)
                start_all(weight_rows(turn, zero()))

            @pl.when(t == tick + 1)
            def _(turn=turn):
                wait_own(turn)

            @pl.when((t > tick) & (t <= tick + n_steps))
            def _(turn=turn, tick=tick, n_steps=n_steps):
                norm_grad(turn, t - tick - 1, n_steps)

        @pl.when(t == OWN_IN + N_PART // 2 + 1)
        def _():
            mine = pltpu.make_async_copy(part_buf, parts.at[me], rows_sem)
            mine.start()
            mine.wait()
            lax.fori_loop(1, N_DEV, send_gain, 0)
            input_grad()
            start_own(2)
            start_all(out_rows(zero()))

        @pl.when(t == OUT_IN)
        def _():
            wait_own(2)

        @pl.when((t >= OUT_IN) & (t < OUT_IN + N_OUT))
        def _():
            out_part(t - OUT_IN)

        n_end = jnp.minimum(jnp.minimum(n + 1, loaded * N_TILE), n_own)
        lax.fori_loop(n, n_end, tile, 0)
        return n_end, loaded + load.astype(jnp.int32)

    n, _ = loop(LAST + 1, body, (zero(), zero()))
    start_own(3)
    for j in range(n_cols):
        sum_ref[:, j * BLK:(j + 1) * BLK] = s_buf[j, :LANES, :]
    lax.fori_loop(n, n_own, tile, 0)
    all_gains().wait_recv()
    dgain_ref[ALL] = jnp.sum(parts[ALL], axis=0)
    for slot in range(TRIO):
        keep_tile(0, slot).wait()
        give_tile(0, slot).wait_send()

    def received(n, carry):
        give_tile(n, 0).wait_recv()
        return carry

    loop(n_own, received, 0)
    wait_own(3)
    for copy in key_copies(pl.ds(0, QROWS)):
        copy.wait_send()
    all_gains().wait_send()


def main(x, dy, gain, pos, freq, w_q, w_k, w_v, w_o):
    model = x.shape[1]
    qkv = w_q.shape[1] + w_k.shape[1] + w_v.shape[1]
    queries, keys = pltpu.VMEM((TRIO, QROWS, LANES), BF16), pltpu.VMEM((SEQ, LANES), BF16)
    return pl.pallas_call(
        main_kernel,
        out_shape=[like((PAIR, *GRID) + x.shape, BF16), like((*GRID, 8, LANES), F32),
                   like((N_PIECE, PAIR, QUAD, PAIR, PAIR, QROWS, LANES), BF16), like((N_GATHER, BLK, BLK), F32),
                   like((LANES, model // 3), BF16), like(x.shape, F32), like(x.shape, BF16), like((PAIR * N_PART, LANES), F32)],
        in_specs=[vmem_spec()] * 5 + [any_spec()] * 4,
        out_specs=[any_spec()] * 4 + [vmem_spec()] * 4,
        scratch_shapes=[
            pltpu.VMEM(x.shape, BF16), queries, queries, keys, keys,
            pltpu.VMEM((*GRID, CHUNK, model), BF16), pltpu.VMEM((8, LANES), F32), pltpu.VMEM((1, model), F32), pltpu.VMEM((1, LANES), F32),
            pltpu.VMEM((*GRID, 8, LANES), F32), pltpu.VMEM((PAIR, LANES, LANES), F32), pltpu.VMEM((N_DEV * CHUNK, LANES), F32),
            pltpu.VMEM((QROWS, LANES), F32), pltpu.VMEM((8, LANES, TRIO * LANES), BF16),
            pltpu.VMEM((PAIR, 3, QROWS, LANES), BF16), pltpu.VMEM((LANES, SEQ), F32), pltpu.VMEM((LANES, SEQ), F32),
            pltpu.VMEM((SEQ // BLK, BLK, BLK), F32), pltpu.VMEM((TRIO, BLK, LANES), F32),
            pltpu.VMEM((QUAD, PAIR, QROWS, LANES), BF16), pltpu.VMEM((TRIO, 2, QROWS, LANES), BF16),
            pltpu.VMEM((PAIR, SEQ, BLK), BF16), pltpu.VMEM((PAIR, *GRID, LANES, BLK), BF16), pltpu.VMEM((TRIO, BLK, BLK), F32),
            pltpu.VMEM((LANES, qkv), BF16), pltpu.VMEM((LANES, PAIR * w_k.shape[1]), BF16), pltpu.VMEM((PAIR, HALF, qkv), BF16), pltpu.VMEM(x.shape, F32),
            pltpu.VMEM((PAIR * N_PART, LANES), F32), pltpu.VMEM((N_DEV, PAIR * N_PART, LANES), F32),
            sems(1, N_SLOT), sems(1, N_SLOT), sems(RING, N_SLOT), sems(RING, N_SLOT),
            sems(TRIO), sems(TRIO), sems(), sems(8), sems(8),
            sems(N_PIECE, 2), sems(PAIR), sems(PAIR), sems(TRIO), sems(TRIO),
            sems(IN_GATHER * N_TILE), sems(TRIO), sems(TRIO), sems(QUAD), sems(PAIR, 4), sems(), sems()],
        compiler_params=pltpu.CompilerParams(collective_id=0, has_side_effects=True, vmem_limit_bytes=VMEM_LIMIT),
    )(x, dy, gain, pos, freq, w_q, w_k, w_v, w_o)


N_LATE = N_PIECE - IN_GATHER
GROUP = IN_GATHER // N_LATE


def finish_kernel(sum_ref, o_ref, dx_ref, dgain_ref, w_ref, hd_ref, g_ref, t_ref,
                  y_ref, dx_out, dgain_out, wq_ref, wk_ref, wv_ref, wo_ref,
                  gbuf, abuf, obuf, cbuf, acc, wbuf, gsem, asem, osem, isem, csem, wsem):
    n_step, group = N_LATE * PER_PIECE, GROUP

    def operand(t):
        return operand_copy(hd_ref, abuf, asem, 1, t, odd(t))

    def cut(t):
        return pl.ds(pl.multiple_of(t * BLK, BLK), BLK)

    def lanes(i):
        return pl.ds(pl.multiple_of(i * LANES, LANES), LANES)

    def to_output(p, t, sub, src, sem):
        j = jnp.where(p == O_PIECES[0], 0, p - O_PIECES[0] - 2)
        return [pltpu.make_async_copy(
            src.at[pl.ds(i * LANES, LANES), :], wo_ref.at[lanes(TRIO * (sub * 4 + i) + j), cut(t)], sem.at[i])
            for i in range(QUAD)]

    def to_input(dst, place, t, sub, src, sem):
        return [pltpu.make_async_copy(
            src.at[:, pl.ds(i * LANES, LANES)], dst.at[cut(t), lanes(place(sub * 4 + i))], sem.at[i]) for i in range(QUAD)]

    def ins(n):
        return [pltpu.make_async_copy(t_ref.at[n * group + i], cbuf.at[lax.rem(n, TRIO), i], isem.at[lax.rem(n, TRIO), i])
                for i in range(group)]

    def start_outs(n):
        for i in range(group):
            m = n * group + i
            p, t, sub = lax.div(m, PER_PIECE), lax.rem(half_of(m), N_TILE), odd(m)
            src, sem = cbuf.at[lax.rem(n, TRIO), i], csem.at[lax.rem(n, TRIO), i]
            for cond, copies in (
                (p < 3, lambda: to_input(wq_ref, lambda g: TRIO * g + p, t, sub, src, sem)),
                (p == KEY_PIECE, lambda: to_input(wk_ref, lambda g: g, t, sub, src, sem)),
                (p == KEY_PIECE + 1, lambda: to_input(wv_ref, lambda g: g, t, sub, src, sem)),
                ((p == O_PIECES[0]) | (p == O_PIECES[1]), lambda: to_output(p, t, sub, src, sem)),
            ):
                @pl.when(cond)
                def _(copies=copies):
                    for c in copies():
                        c.start()

    def wait_outs(n):
        for i in range(group):
            for c in to_output(IN_GATHER, 0, 0, cbuf.at[0, i], csem.at[lax.rem(n, TRIO), i]):
                c.wait()

    def weight(i):
        slot = odd(i)
        return pltpu.make_async_copy(w_ref.at[lanes(TRIO * i + 2), :], wbuf.at[slot], wsem.at[slot])

    for late in range(N_LATE):
        for sub in range(PAIR):
            start_all(piece_copies(g_ref, gbuf, gsem, IN_GATHER + late, sub, late * 2 + sub))
    operand(zero()).start()
    weight(zero()).start()
    acc[ALL] = sum_ref[ALL]
    dx_out[ALL] = dx_ref[ALL]
    dgain_out[ALL] = dgain_ref[ALL]

    def step(n, carry):
        t, late, sub = lax.div(n, PAIR * N_LATE), lax.rem(half_of(n), N_LATE), odd(n)
        p, held = IN_GATHER + late, late * 2 + sub
        slot = lax.rem(n, TRIO)

        @pl.when(n >= 3)
        def _():
            wait_outs(n - 3)
        for c in ins(n):
            c.start()

        @pl.when(n >= 1)
        def _():
            for c in ins(n - 1):
                c.wait()
            start_outs(n - 1)

        @pl.when(held == 0)
        def _():
            operand(t).wait()

            @pl.when(nxt(t) < N_TILE)
            def _():
                operand(nxt(t)).start()

        @pl.when(n < PAIR * N_LATE)
        def _():
            wait_piece(gbuf, gsem, held)

        @pl.when(n >= 3)
        def _():
            for c in to_output(IN_GATHER, 0, 0, obuf.at[0], osem.at[slot]):
                c.wait()
        @pl.when(n < 8)
        def _():
            weight(n).wait()

            @pl.when(n < 7)
            def _():
                weight(n + 1).start()
            acc[ALL] += jnp.dot(o_ref[:, lanes(n)], wbuf[odd(n)], preferred_element_type=F32)
        obuf[slot] = tile_product(abuf[odd(t)], gbuf[held], True)
        for c in to_output(p, t, sub, obuf.at[slot], osem.at[slot]):
            c.start()
        return carry

    loop(n_step, step, 0)
    y_ref[ALL] = acc[ALL].astype(BF16)
    for c in ins(n_step - 1):
        c.wait()
    start_outs(jnp.int32(n_step - 1))
    for n in range(n_step - 3, n_step):
        wait_outs(n)
        for c in to_output(IN_GATHER, 0, 0, obuf.at[0], osem.at[n % 3]):
            c.wait()


def finish(x, o, dx, dgain, w_o, hd, g, tiles):
    model, kv = hd.shape[2], 8 * LANES
    return pl.pallas_call(
        finish_kernel,
        out_shape=[like(x.shape, BF16), like(dx.shape, BF16), like(dgain.shape, F32)]
        + [like((model, n), F32) for n in (TRIO * kv, kv, kv)] + [like((TRIO * kv, model), F32)],
        in_specs=[vmem_spec()] * 4 + [any_spec()] * 4,
        out_specs=[vmem_spec()] * 3 + [any_spec()] * 4,
        scratch_shapes=[pltpu.VMEM((PAIR * N_LATE, SEQ, BLK), BF16), pltpu.VMEM((PAIR, SEQ, BLK), BF16), pltpu.VMEM((TRIO, BLK, BLK), F32),
                        pltpu.VMEM((TRIO, GROUP, BLK, BLK), F32), pltpu.VMEM(x.shape, F32), pltpu.VMEM((PAIR, LANES, model), BF16),
                        sems(PAIR * N_LATE), sems(PAIR), sems(TRIO, 4), sems(TRIO, GROUP), sems(TRIO, GROUP, 4), sems(PAIR)],
        cost_estimate=pl.CostEstimate(flops=4 * SEQ * kv * model, bytes_accessed=250 * 2**20, transcendentals=0),
        compiler_params=pltpu.CompilerParams(vmem_limit_bytes=VMEM_LIMIT),
    )(x, o, dx, dgain, w_o, hd, g, tiles)


def solution(mesh):
    assert mesh.shape['hp'] == 4 and mesh.shape['cp'] == 8

    def device_step(hidden, grad_out, positions, norm_gain, w_q, w_k, w_v, w_o, inv_freq):
        model = hidden.shape[1]
        hd, _, gathered, tiles, o_own, total, dx, gains = main(
            hidden, grad_out, norm_gain, positions, inv_freq, w_q, w_k, w_v, w_o)
        output, grad_hidden, grad_gain, grad_wq, grad_wk, grad_wv, grad_wo = finish(
            total, o_own, dx, gains, w_o, hd.reshape(2, SEQ, model), gathered, tiles)
        grad_gain = grad_gain.reshape(-1)
        return output, grad_hidden, grad_wq, grad_wk, grad_wv, grad_wo, grad_gain

    rows, whole = P(('cp', 'hp'), None), P()
    return jax.shard_map(
        device_step, mesh=mesh,
        in_specs=(rows, rows, P(('cp', 'hp')), whole, whole, whole, whole, whole, whole),
        out_specs=(rows, rows, whole, whole, whole, whole, whole), check_vma=False)
```

time: 1840 us -> 586 us (0.32)
  waiting for transfers between devices: 1370 us -> 0 us
  Pallas kernels: 0 us -> 585 us
  matrix products: 229 us -> 0 us
  local copies, waits for them, and re-layouts: 106 us -> 0 us
  blocking collectives: 41.7 us -> 0 us
  other arithmetic: 40.1 us -> 0 us
  starting transfers between devices: 35 us -> 0 us
    psum x1 -> x0, waiting for transfers between devices: 1310 us -> none  [device_step(): lax.psum((grad_wq, grad_wk, grad_wv, grad_wo, grad_gain), ('hp', 'cp'))]
    pallas_call x0 -> x2, Pallas kernels: none -> 585 us  [the longest x1 507 us: main(): pl.pallas_call(main_kernel, out_shape=[like((PAIR, *GRID) + x.shape, BF16...]
    dot_general x16 -> x0, matrix products: 198 us -> none  [the longest x1 38.3 us: device_step(): jnp.einsum('qkgd,tkd->kgqt', do_head, v_all, preferred_element_type=jnp.f...]
    unnamed x50 -> x0, local copies, waits for them, and re-layouts: 84.2 us -> none
    all_to_all x8 -> x0, waiting for transfers between devices: 54.2 us -> none  [the longest x1 17.4 us: device_step(): lax.all_to_all(out_head.reshape(pair_rows, loc_heads, head_dim), 'hp', 0,...]
    psum x1 -> x0, blocking collectives: 41.7 us -> none  [device_step(): lax.psum((grad_wq, grad_wk, grad_wv, grad_wo, grad_gain), ('hp', 'cp'))]
    all_to_all x8 -> x0, starting transfers between devices: 34.9 us -> none  [the longest x1 6.38 us: device_step(): k_head = lax.all_to_all(k_rot, 'hp', 1, 0, tiled=True)]
    convert_element_type x5 -> x0, other arithmetic: 30.4 us -> none  [the longest x1 26.1 us: device_step(): prob_b16 = prob_f32.astype(jnp.bfloat16)]
  transfers between devices with their start and end apart: 13 -> 0, of which waited for: 6 -> 0; matrix products, arithmetic and copies ran while one was open for 14% -> 0% of each run, Pallas kernels for 0% -> 0%
where the time goes in v2:
time: 586 us
  Pallas kernels  585 us (100%)
    pallas_call x1, Pallas kernels, main(): pl.pallas_call(main_kernel, out_shape=[like((PAIR, *GRID) + x.shape, BF16...  507 us
    pallas_call x1, Pallas kernels, finish(): pl.pallas_call(finish_kernel, out_shape=[like(x.shape, BF16), like(dx.sha...  77.4 us

profile of v2, /device:TPU:0, one launch (start us, length us, event | category | flops | bytes accessed | tf_op | source)
XLA Modules:
  0.0 585.7 jit_solution(8014525032454398410)
XLA Ops:
  0.6 507.5 %shard_map.144 = (bf16[2,2,2,2,4,128,3072]{6,5,4,3,2,1,0:T(8,128)(2,1)}, f32[2,2,2,4,8,128]{5,4,3,2,1,0:T(8,128)}, bf16[8,2,4,2,2,1024,128]{6,5,4,3,2,1,0:T(8,12...) custom-call(bf16[128,3072]{1,0:T(8,128)(2,1)} %x_ref.1, ...), custom_call_target="tpu_custom_call" | custom-call | tf_op jit(solution)/shard_map/pallas_call | solution.py:813
  508.1 77.4 %shard_map.145 = (bf16[128,3072]{1,0:T(8,128)(2,1)}, bf16[128,3072]{1,0:T(8,128)(2,1)}, f32[24,128]{1,0:T(8,128)}, f32[3072,3072]{1,0:T(8,128)}, f32[3072,1024]{...) custom-call(f32[128,3072]{1,0:T(8,128)} %get-tuple-element.21.sum_ref, ...), custom_call_target="tpu_custom_call" | custom-call | flops 51539607552 | bytes 262144000 | tf_op jit(solution)/shard_map/pallas_call | solution.py:964

commit v3 on v2

--- a/solution.py
+++ b/solution.py
@@ -59,8 +59,8 @@
 
 
 class Gather:
-    def __init__(self, send_sem, recv_sem, period, base=0):
-        self.period, self.base = period, base
+    def __init__(self, send_sem, recv_sem, mix, base=0):
+        self.mix, self.base = mix, base
         self.z = lax.axis_index('hp')
         cp = lax.axis_index('cp')
         self.c, self.x, self.y = odd(cp), odd(half_of(cp)), lax.div(cp, 4)
@@ -129,9 +129,12 @@
                 self.run(sem_row, kind, view, stage, 'sent')
 
     def kinds(self, u):
-        w, even = lax.rem(u, self.period), odd(u) == 0
-        e, f = w == 0, w == self.period - 5
-        return (('C', ~(e | f) & even), ('D', ~(e | f) & ~even), ('E', e), ('F', f))
+        word, at = lax.div(u, 16), lax.rem(u, 16)
+        code = jnp.int32(self.mix[0])
+        for i in range(1, len(self.mix)):
+            code = jnp.where(word == i, self.mix[i], code)
+        code = lax.shift_right_logical(code, at * 2) & 3
+        return tuple((kind, code == i) for i, kind in enumerate('CDEF'))
 
     def tick(self, t, n_units, view):
         for s in range(N_STAGE + 2):
@@ -350,7 +353,7 @@
                 piece_buf, dk_acc, dv_acc, s_buf, state, dkv_buf, peer_buf, gbuf, abuf, obuf, own_buf, oo_buf, w_buf, dn_buf, part_buf, parts,
                 cs_send, cs_recv, send_sem, recv_sem, first_sem, proj_sem, rows_sem, do_send, do_recv,
                 lsem, gsem, asem, osem, tsend, trecv, psend, precv, rsem, wsem, gain_send, gain_recv):
-    net_in, net_cs, net = Gather(send_sem, recv_sem, 9), Gather(cs_send, cs_recv, 9), Gather(send_sem, recv_sem, 8, START)
+    net_in, net_cs, net = Gather(send_sem, recv_sem, (293880977, 1175604295)), Gather(cs_send, cs_recv, (293880977, 1175604295)), Gather(send_sem, recv_sem, (-398134202, 303174049, 1212958790, -1471626106), START)
     quarter = net.y * 2 + net.x
     head = net.c * 4 + net.z
     spot = (net.y, net.x, net.c, net.z)

time: 586 us -> 563 us (0.961)
  Pallas kernels: 585 us -> 562 us
    pallas_call x1, Pallas kernels: 507 us -> 484 us  [main(): pl.pallas_call(main_kernel, out_shape=[like((PAIR, *GRID) + x.shape, BF16...]
where the time goes in v3:
time: 563 us; the launch traced here: 562 us
  Pallas kernels  562 us (100%)
    pallas_call x1, Pallas kernels, main(): pl.pallas_call(main_kernel, out_shape=[like((PAIR, *GRID) + x.shape, BF16...  484 us
    pallas_call x1, Pallas kernels, finish(): pl.pallas_call(finish_kernel, out_shape=[like(x.shape, BF16), like(dx.sha...  77.4 us

profile of v3, /device:TPU:0, one launch (start us, length us, event | category | flops | bytes accessed | tf_op | source)
XLA Modules:
  0.0 562.4 jit_solution(1092546953256420498)
XLA Ops:
  0.6 484.1 %shard_map.144 = (bf16[2,2,2,2,4,128,3072]{6,5,4,3,2,1,0:T(8,128)(2,1)}, f32[2,2,2,4,8,128]{5,4,3,2,1,0:T(8,128)}, bf16[8,2,4,2,2,1024,128]{6,5,4,3,2,1,0:T(8,12...) custom-call(bf16[128,3072]{1,0:T(8,128)(2,1)} %x_ref.1, ...), custom_call_target="tpu_custom_call" | custom-call | tf_op jit(solution)/shard_map/pallas_call | solution.py:816
  484.8 77.4 %shard_map.145 = (bf16[128,3072]{1,0:T(8,128)(2,1)}, bf16[128,3072]{1,0:T(8,128)(2,1)}, f32[24,128]{1,0:T(8,128)}, f32[3072,3072]{1,0:T(8,128)}, f32[3072,1024]{...) custom-call(f32[128,3072]{1,0:T(8,128)} %get-tuple-element.21.sum_ref, ...), custom_call_target="tpu_custom_call" | custom-call | flops 51539607552 | bytes 262144000 | tf_op jit(solution)/shard_map/pallas_call | solution.py:967

commit v4 on v3

--- a/solution.py
+++ b/solution.py
@@ -33,9 +33,7 @@
     'E': ('x', 'y', 'z1', 'z2', 'z3', 'd'),
     'F': ('y', 'x', 'z1', 'z2', 'z3', 'd'),
 }
-SLOT = {'z1': 0, 'z2': 2, 'z3': 4, 'x': 6, 'y': 7, 'd': 8}
 N_STAGE = 6
-N_SLOT = 9
 
 
 def odd(i):
@@ -76,45 +74,46 @@
         done = {st[0] for st in order[:order.index(stage)]}
         every = EVERY
         gx, gy, gz = (every if d in done else v for d, v in (('x', x), ('y', y), ('z', z)))
-        slot = SLOT[stage]
-
-        def copy(place, device, slot):
+        slot = order.index(stage)
+
+        def copy(place, device):
             return lambda: pltpu.make_async_remote_copy(
                 place, place, self.send_sem.at[sem_row, slot], self.recv_sem.at[sem_row, slot],
                 device_id=device, device_id_type=pl.DeviceIdType.MESH)
 
-        if stage == 'x':
-            dev = self.device(x=1 - x)
-            return [(None, copy(view(c, x, gy, gz), dev, slot), None, copy(view(c, 1 - x, gy, gz), dev, slot))]
-        if stage == 'y':
-            dev = self.device(y=1 - y)
-            return [(None, copy(view(c, gx, y, gz), dev, slot), None, copy(view(c, gx, 1 - y, gz), dev, slot))]
-        if stage == 'd':
-            dev = self.device(c=1 - c)
-            return [(None, copy(view(c, every, every, every), dev, slot),
-                     None, copy(view(1 - c, every, every, every), dev, slot))]
+        if stage in 'xyd':
+            mine, other, dev = {
+                'x': lambda: ((c, x, gy, gz), (c, 1 - x, gy, gz), self.device(x=1 - x)),
+                'y': lambda: ((c, gx, y, gz), (c, gx, 1 - y, gz), self.device(y=1 - y)),
+                'd': lambda: ((c, EVERY, EVERY, EVERY), (1 - c, EVERY, EVERY, EVERY), self.device(c=1 - c)),
+            }[stage]()
+            out, back = [(True, copy(view(*mine), dev))], [(True, copy(view(*other), dev))]
+            return {'start': out, 'sent': out, 'recv': back}
         hop = int(stage[1])
-        up, down = self.device(z=jnp.minimum(z + 1, 3)), self.device(z=jnp.maximum(z - 1, 0))
-        return [
-            ((z >= hop - 1) & (z < 3), copy(view(c, gx, gy, jnp.maximum(z - hop + 1, 0)), up, slot),
-             z >= hop, copy(view(c, gx, gy, jnp.maximum(z - hop, 0)), up, slot)),
-            ((z + hop <= 4) & (z > 0), copy(view(c, gx, gy, jnp.minimum(z + hop - 1, 3)), down, slot + 1),
-             z + hop <= 3, copy(view(c, gx, gy, jnp.minimum(z + hop, 3)), down, slot + 1)),
-        ]
+        ups, downs = (z >= hop - 1) & (z < 3), (z + hop <= 4) & (z > 0)
+        above, below = self.device(z=jnp.minimum(z + 1, 3)), self.device(z=jnp.maximum(z - 1, 0))
+
+        def counted(one, other):
+            return [(one != other, copy(view(c, gx, gy, 0), above)), (one & other, copy(view(c, gx, gy, pl.ds(0, PAIR)), above))]
+
+        return {
+            'start': [(ups, copy(view(c, gx, gy, jnp.maximum(z - hop + 1, 0)), above)),
+                      (downs, copy(view(c, gx, gy, jnp.minimum(z + hop - 1, 3)), below))],
+            'sent': counted(ups, downs),
+            'recv': counted(z >= hop, z + hop <= 3),
+        }
 
     def run(self, sem_row, kind, view, stage, what):
-        for can_send, send, can_recv, recv in self.copies(sem_row, kind, view, stage):
-            cond = can_recv if what == 'recv' else can_send
-
-            def act(send=send, recv=recv):
+        for cond, copy in self.copies(sem_row, kind, view, stage)[what]:
+            def act(copy=copy):
                 if what == 'start':
-                    send().start()
+                    copy().start()
                 elif what == 'sent':
-                    send().wait_send()
+                    copy().wait_send()
                 else:
-                    recv().wait_recv()
-
-            if cond is None:
+                    copy().wait_recv()
+
+            if cond is True:
                 act()
             else:
                 pl.when(cond)(act)
@@ -350,7 +349,7 @@
 def main_kernel(x_ref, dy_ref, gain_ref, mypos_ref, freq_ref, wq_ref, wk_ref, wv_ref, wo_ref,
                 hd_ref, pos_ref, g_ref, t_ref, o_ref, sum_ref, dx_ref, dgain_ref,
                 h_buf, q_buf, do_buf, k_buf, v_buf, rows_buf, mypos_buf, gain_buf, freq_buf, pos_buf, pos_t, cs_buf, own_cs, do_parts,
-                piece_buf, dk_acc, dv_acc, s_buf, state, dkv_buf, peer_buf, gbuf, abuf, obuf, own_buf, oo_buf, w_buf, dn_buf, part_buf, parts,
+                piece_buf, dk_acc, dv_acc, s_buf, state, dkv_buf, peer_buf, gbuf, abuf, obuf, own_buf, oo_buf, w_buf, dn_buf, part_buf, z_parts, sum_buf, parts,
                 cs_send, cs_recv, send_sem, recv_sem, first_sem, proj_sem, rows_sem, do_send, do_recv,
                 lsem, gsem, asem, osem, tsend, trecv, psend, precv, rsem, wsem, gain_send, gain_recv):
     net_in, net_cs, net = Gather(send_sem, recv_sem, (293880977, 1175604295)), Gather(cs_send, cs_recv, (293880977, 1175604295)), Gather(send_sem, recv_sem, (-398134202, 303174049, 1212958790, -1471626106), START)
@@ -363,19 +362,23 @@
         x = x_ref[ALL].astype(F32)
         return lax.rsqrt(jnp.mean(x * x, **BY_ROW) + NORM_EPS)
 
-    me = lax.axis_index('cp') * 4 + net.z
-
-    def device_at(step):
-        other = lax.rem(me + step, N_DEV)
-        return lax.rem(other, 4), lax.div(other, 4)
-
     barrier = pltpu.get_barrier_semaphore()
 
-    def greet(step, carry):
-        pl.semaphore_signal(barrier, inc=1, device_id=device_at(step), device_id_type=pl.DeviceIdType.MESH)
-        return carry
-
-    lax.fori_loop(1, N_DEV, greet, 0)
+    def greet(**moved):
+        pl.semaphore_signal(barrier, inc=1, device_id=net.device(**moved), device_id_type=pl.DeviceIdType.MESH)
+
+    greet(x=1 - net.x)
+    greet(y=1 - net.y)
+    greet(c=1 - net.c)
+    inner = (net.z > 0).astype(jnp.int32) + (net.z < 3).astype(jnp.int32)
+
+    @pl.when(net.z > 0)
+    def _():
+        greet(z=net.z - 1)
+
+    @pl.when(net.z < 3)
+    def _():
+        greet(z=net.z + 1)
 
     gain_buf[ALL] = gain_ref[ALL].astype(F32).reshape(gain_buf.shape)
     freq_buf[ALL] = jnp.concatenate([freq_ref[ALL], freq_ref[ALL]], axis=0).reshape(freq_buf.shape)
@@ -385,7 +388,7 @@
         (h_buf, hd_ref.at[(0, *spot)]), (dy_ref, hd_ref.at[(1, *spot)]), (mypos_buf, pos_ref.at[spot])))]
     start_all(first)
     wait_all(first)
-    pl.semaphore_wait(barrier, N_DEV - 1)
+    pl.semaphore_wait(barrier, TRIO + inner)
     q_cols = pl.ds(pl.multiple_of(head * TRIO * LANES, LANES), TRIO * LANES)
     kv_cols = pl.ds(pl.multiple_of(head * LANES, LANES), LANES)
     w_rows = slice(0, wq_ref.shape[0])
@@ -622,16 +625,33 @@
             for k in range(PAIR):
                 part_buf[pl.ds(block * 2 + k, 1), :] = total[:, k * LANES:(k + 1) * LANES]
 
-    def send_gain(step, carry):
-        pltpu.make_async_remote_copy(
-            part_buf, parts.at[me], gain_send, gain_recv,
-            device_id=device_at(step), device_id_type=pl.DeviceIdType.MESH).start()
-        return carry
-
-    def all_gains():
-        rest = parts.at[pl.ds(1, N_DEV - 1)]
+    column = (net.y * PAIR + net.x) * PAIR + net.c
+
+    def share(src, dst, slot, n, sem, device):
+        def send(step, carry):
+            pltpu.make_async_remote_copy(
+                src, dst.at[slot], gain_send.at[sem], gain_recv.at[sem],
+                device_id=device(lax.rem(slot + step, n)), device_id_type=pl.DeviceIdType.MESH).start()
+            return carry
+
+        mine = pltpu.make_async_copy(src, dst.at[slot], rows_sem)
+        mine.start()
+        mine.wait()
+        lax.fori_loop(1, n, send, 0)
+
+    def shared(dst, n, sem):
+        rest = dst.at[pl.ds(1, n - 1)]
         return pltpu.make_async_remote_copy(
-            rest, rest, gain_send, gain_recv, device_id=net.device(c=1 - net.c), device_id_type=pl.DeviceIdType.MESH)
+            rest, rest, gain_send.at[sem], gain_recv.at[sem],
+            device_id=net.device(c=1 - net.c), device_id_type=pl.DeviceIdType.MESH)
+
+    def gain_column():
+        share(part_buf, z_parts, net.z, QUAD, 0, lambda z: net.device(z=z))
+
+    def gain_rest():
+        shared(z_parts, QUAD, 0).wait_recv()
+        sum_buf[ALL] = jnp.sum(z_parts[ALL], axis=0)
+        share(sum_buf, parts, column, 8, 1, lambda k: (net.z, k))
 
     def input_grad():
         x_hat = x_ref[ALL].astype(F32) * inv_rms()
@@ -767,10 +787,7 @@
 
         @pl.when(t == OWN_IN + N_PART // 2 + 1)
         def _():
-            mine = pltpu.make_async_copy(part_buf, parts.at[me], rows_sem)
-            mine.start()
-            mine.wait()
-            lax.fori_loop(1, N_DEV, send_gain, 0)
+            gain_column()
             input_grad()
             start_own(2)
             start_all(out_rows(zero()))
@@ -778,6 +795,7 @@
         @pl.when(t == OUT_IN)
         def _():
             wait_own(2)
+            gain_rest()
 
         @pl.when((t >= OUT_IN) & (t < OUT_IN + N_OUT))
         def _():
@@ -792,7 +810,7 @@
     for j in range(n_cols):
         sum_ref[:, j * BLK:(j + 1) * BLK] = s_buf[j, :LANES, :]
     lax.fori_loop(n, n_own, tile, 0)
-    all_gains().wait_recv()
+    shared(parts, 8, 1).wait_recv()
     dgain_ref[ALL] = jnp.sum(parts[ALL], axis=0)
     for slot in range(TRIO):
         keep_tile(0, slot).wait()
@@ -806,12 +824,14 @@
     wait_own(3)
     for copy in key_copies(pl.ds(0, QROWS)):
         copy.wait_send()
-    all_gains().wait_send()
+    shared(z_parts, QUAD, 0).wait_send()
+    shared(parts, 8, 1).wait_send()
 
 
 def main(x, dy, gain, pos, freq, w_q, w_k, w_v, w_o):
     model = x.shape[1]
     qkv = w_q.shape[1] + w_k.shape[1] + w_v.shape[1]
+    gains = pltpu.VMEM((PAIR * N_PART, LANES), F32)
     queries, keys = pltpu.VMEM((TRIO, QROWS, LANES), BF16), pltpu.VMEM((SEQ, LANES), BF16)
     return pl.pallas_call(
         main_kernel,
@@ -830,11 +850,11 @@
             pltpu.VMEM((QUAD, PAIR, QROWS, LANES), BF16), pltpu.VMEM((TRIO, 2, QROWS, LANES), BF16),
             pltpu.VMEM((PAIR, SEQ, BLK), BF16), pltpu.VMEM((PAIR, *GRID, LANES, BLK), BF16), pltpu.VMEM((TRIO, BLK, BLK), F32),
             pltpu.VMEM((LANES, qkv), BF16), pltpu.VMEM((LANES, PAIR * w_k.shape[1]), BF16), pltpu.VMEM((PAIR, HALF, qkv), BF16), pltpu.VMEM(x.shape, F32),
-            pltpu.VMEM((PAIR * N_PART, LANES), F32), pltpu.VMEM((N_DEV, PAIR * N_PART, LANES), F32),
-            sems(1, N_SLOT), sems(1, N_SLOT), sems(RING, N_SLOT), sems(RING, N_SLOT),
+            gains, pltpu.VMEM((QUAD, PAIR * N_PART, LANES), F32), gains, pltpu.VMEM((8, PAIR * N_PART, LANES), F32),
+            sems(1, N_STAGE), sems(1, N_STAGE), sems(RING, N_STAGE), sems(RING, N_STAGE),
             sems(TRIO), sems(TRIO), sems(), sems(8), sems(8),
             sems(N_PIECE, 2), sems(PAIR), sems(PAIR), sems(TRIO), sems(TRIO),
-            sems(IN_GATHER * N_TILE), sems(TRIO), sems(TRIO), sems(QUAD), sems(PAIR, 4), sems(), sems()],
+            sems(IN_GATHER * N_TILE), sems(TRIO), sems(TRIO), sems(QUAD), sems(PAIR, 4), sems(PAIR), sems(PAIR)],
         compiler_params=pltpu.CompilerParams(collective_id=0, has_side_effects=True, vmem_limit_bytes=VMEM_LIMIT),
     )(x, dy, gain, pos, freq, w_q, w_k, w_v, w_o)
 

time: 563 us -> 556 us (0.988)
  Pallas kernels: 562 us -> 554 us
    pallas_call x1, Pallas kernels: 484 us -> 477 us  [main(): pl.pallas_call(main_kernel, out_shape=[like((PAIR, *GRID) + x.shape, BF16...]
where the time goes in v4:
time: 556 us; the launch traced here: 555 us
  Pallas kernels  554 us (100%)
    pallas_call x1, Pallas kernels, main(): pl.pallas_call(main_kernel, out_shape=[like((PAIR, *GRID) + x.shape, BF16...  477 us
    pallas_call x1, Pallas kernels, finish(): pl.pallas_call(finish_kernel, out_shape=[like(x.shape, BF16), like(dx.sha...  77.4 us

profile of v4, /device:TPU:0, one launch (start us, length us, event | category | flops | bytes accessed | tf_op | source)
XLA Modules:
  0.0 555.0 jit_solution(1305982359133768035)
XLA Ops:
  0.6 476.8 %shard_map.144 = (bf16[2,2,2,2,4,128,3072]{6,5,4,3,2,1,0:T(8,128)(2,1)}, f32[2,2,2,4,8,128]{5,4,3,2,1,0:T(8,128)}, bf16[8,2,4,2,2,1024,128]{6,5,4,3,2,1,0:T(8,12...) custom-call(bf16[128,3072]{1,0:T(8,128)(2,1)} %x_ref.1, ...), custom_call_target="tpu_custom_call" | custom-call | tf_op jit(solution)/shard_map/pallas_call | solution.py:836
  477.5 77.4 %shard_map.145 = (bf16[128,3072]{1,0:T(8,128)(2,1)}, bf16[128,3072]{1,0:T(8,128)(2,1)}, f32[24,128]{1,0:T(8,128)}, f32[3072,3072]{1,0:T(8,128)}, f32[3072,1024]{...) custom-call(f32[128,3072]{1,0:T(8,128)} %get-tuple-element.21.sum_ref, ...), custom_call_target="tpu_custom_call" | custom-call | flops 51539607552 | bytes 262144000 | tf_op jit(solution)/shard_map/pallas_call | solution.py:987

commit v5 on v4

--- a/solution.py
+++ b/solution.py
@@ -340,8 +340,9 @@
 KEYS_IN = START + KEY_PIECE * UPP
 QUERY_IN = START + 3 * UPP + DELAY
 OWN_IN = START + O_PIECES[1] * UPP + DELAY
+QUERIES_DONE = QUERY_IN + N_PART
+FIRST_O = START + (O_PIECES[0] + 1) * UPP + DELAY
 OUT_IN = OWN_IN + N_PART // 2 + 2
-N_OUT = 8
 LAST = START + N_UNIT + DELAY + LAG
 N_DEV = 32
 
@@ -352,7 +353,7 @@
                 piece_buf, dk_acc, dv_acc, s_buf, state, dkv_buf, peer_buf, gbuf, abuf, obuf, own_buf, oo_buf, w_buf, dn_buf, part_buf, z_parts, sum_buf, parts,
                 cs_send, cs_recv, send_sem, recv_sem, first_sem, proj_sem, rows_sem, do_send, do_recv,
                 lsem, gsem, asem, osem, tsend, trecv, psend, precv, rsem, wsem, gain_send, gain_recv):
-    net_in, net_cs, net = Gather(send_sem, recv_sem, (293880977, 1175604295)), Gather(cs_send, cs_recv, (293880977, 1175604295)), Gather(send_sem, recv_sem, (-398134202, 303174049, 1212958790, -1471626106), START)
+    net_in, net_cs, net = Gather(send_sem, recv_sem, (306463953, 1175604295)), Gather(cs_send, cs_recv, (306463953, 1175604295)), Gather(send_sem, recv_sem, (-398134202, 1293043604, -2075179916, 958350436), START)
     quarter = net.y * 2 + net.x
     head = net.c * 4 + net.z
     spot = (net.y, net.x, net.c, net.z)
@@ -580,7 +581,7 @@
 
     kv = wk_ref.shape[1]
     groups = (((0, 1, 2), own_buf, slice(0, TRIO * kv)), ((KEY_PIECE, KEY_PIECE + 1), own_buf, slice(TRIO * kv, 5 * kv)),
-              (O_PIECES[:2], oo_buf, slice(0, PAIR * kv)), (O_PIECES[2:], o_ref, slice(0, kv)))
+              (O_PIECES[:1], oo_buf, slice(0, kv)), (O_PIECES[1:2], oo_buf, slice(kv, PAIR * kv)), (O_PIECES[2:], o_ref, slice(0, kv)))
 
     def start_own(i):
         rows = pl.ds(pl.multiple_of(net.c * BLK + net.z * LANES, LANES), LANES)
@@ -672,7 +673,7 @@
         slot = odd(i)
         wait_all(out_rows(i))
 
-        @pl.when(nxt(i) < N_OUT)
+        @pl.when(lax.rem(i, QUAD) < 3)
         def _():
             start_all(out_rows(nxt(i)))
         left = oo_buf[:, part(i)]
@@ -789,24 +790,35 @@
         def _():
             gain_column()
             input_grad()
+            start_own(3)
+            start_all(out_rows(jnp.int32(QUAD)))
+
+        @pl.when(t == FIRST_O)
+        def _():
             start_own(2)
+
+        @pl.when(t == QUERIES_DONE)
+        def _():
+            wait_own(2)
             start_all(out_rows(zero()))
 
         @pl.when(t == OUT_IN)
         def _():
-            wait_own(2)
+            wait_own(3)
             gain_rest()
 
-        @pl.when((t >= OUT_IN) & (t < OUT_IN + N_OUT))
-        def _():
-            out_part(t - OUT_IN)
+        early = (t > QUERIES_DONE) & (t <= QUERIES_DONE + QUAD)
+
+        @pl.when(early | ((t >= OUT_IN) & (t < OUT_IN + QUAD)))
+        def _():
+            out_part(jnp.where(early, t - QUERIES_DONE - 1, t - OUT_IN + QUAD))
 
         n_end = jnp.minimum(jnp.minimum(n + 1, loaded * N_TILE), n_own)
         lax.fori_loop(n, n_end, tile, 0)
         return n_end, loaded + load.astype(jnp.int32)
 
     n, _ = loop(LAST + 1, body, (zero(), zero()))
-    start_own(3)
+    start_own(4)
     for j in range(n_cols):
         sum_ref[:, j * BLK:(j + 1) * BLK] = s_buf[j, :LANES, :]
     lax.fori_loop(n, n_own, tile, 0)
@@ -821,7 +833,7 @@
         return carry
 
     loop(n_own, received, 0)
-    wait_own(3)
+    wait_own(4)
     for copy in key_copies(pl.ds(0, QROWS)):
         copy.wait_send()
     shared(z_parts, QUAD, 0).wait_send()
@@ -854,7 +866,7 @@
             sems(1, N_STAGE), sems(1, N_STAGE), sems(RING, N_STAGE), sems(RING, N_STAGE),
             sems(TRIO), sems(TRIO), sems(), sems(8), sems(8),
             sems(N_PIECE, 2), sems(PAIR), sems(PAIR), sems(TRIO), sems(TRIO),
-            sems(IN_GATHER * N_TILE), sems(TRIO), sems(TRIO), sems(QUAD), sems(PAIR, 4), sems(PAIR), sems(PAIR)],
+            sems(IN_GATHER * N_TILE), sems(TRIO), sems(TRIO), sems(5), sems(PAIR, 4), sems(PAIR), sems(PAIR)],
         compiler_params=pltpu.CompilerParams(collective_id=0, has_side_effects=True, vmem_limit_bytes=VMEM_LIMIT),
     )(x, dy, gain, pos, freq, w_q, w_k, w_v, w_o)
 

time: 556 us -> 552 us (level)
  no operation moved by 1% of the time
where the time goes in v5:
time: 552 us; the launch traced here: 551 us
  Pallas kernels  550 us (100%)
    pallas_call x1, Pallas kernels, main(): pl.pallas_call(main_kernel, out_shape=[like((PAIR, *GRID) + x.shape, BF16...  473 us
    pallas_call x1, Pallas kernels, finish(): pl.pallas_call(finish_kernel, out_shape=[like(x.shape, BF16), like(dx.sha...  77.4 us

profile of v5, /device:TPU:0, one launch (start us, length us, event | category | flops | bytes accessed | tf_op | source)
XLA Modules:
  0.0 551.1 jit_solution(9510258084824862392)
XLA Ops:
  0.6 472.9 %shard_map.144 = (bf16[2,2,2,2,4,128,3072]{6,5,4,3,2,1,0:T(8,128)(2,1)}, f32[2,2,2,4,8,128]{5,4,3,2,1,0:T(8,128)}, bf16[8,2,4,2,2,1024,128]{6,5,4,3,2,1,0:T(8,12...) custom-call(bf16[128,3072]{1,0:T(8,128)(2,1)} %x_ref.1, ...), custom_call_target="tpu_custom_call" | custom-call | tf_op jit(solution)/shard_map/pallas_call | solution.py:848
  473.5 77.4 %shard_map.145 = (bf16[128,3072]{1,0:T(8,128)(2,1)}, bf16[128,3072]{1,0:T(8,128)(2,1)}, f32[24,128]{1,0:T(8,128)}, f32[3072,3072]{1,0:T(8,128)}, f32[3072,1024]{...) custom-call(f32[128,3072]{1,0:T(8,128)} %get-tuple-element.21.sum_ref, ...), custom_call_target="tpu_custom_call" | custom-call | flops 51539607552 | bytes 262144000 | tf_op jit(solution)/shard_map/pallas_call | solution.py:999

commit v6 on v5

--- a/solution.py
+++ b/solution.py
@@ -57,8 +57,8 @@
 
 
 class Gather:
-    def __init__(self, send_sem, recv_sem, mix, base=0):
-        self.mix, self.base = mix, base
+    def __init__(self, send_sem, recv_sem, mix, base=0, source=lambda u: ()):
+        self.mix, self.base, self.source, self.unit = mix, base, source, 0
         self.z = lax.axis_index('hp')
         cp = lax.axis_index('cp')
         self.c, self.x, self.y = odd(cp), odd(half_of(cp)), lax.div(cp, 4)
@@ -76,10 +76,12 @@
         gx, gy, gz = (every if d in done else v for d, v in (('x', x), ('y', y), ('z', z)))
         slot = order.index(stage)
 
-        def copy(place, device):
+        def copy(place, device, src=()):
             return lambda: pltpu.make_async_remote_copy(
-                place, place, self.send_sem.at[sem_row, slot], self.recv_sem.at[sem_row, slot],
+                place if isinstance(src, tuple) else src, place, self.send_sem.at[sem_row, slot], self.recv_sem.at[sem_row, slot],
                 device_id=device, device_id_type=pl.DeviceIdType.MESH)
+
+        first = self.source(self.unit) if slot == 0 else ()
 
         if stage in 'xyd':
             mine, other, dev = {
@@ -88,7 +90,8 @@
                 'd': lambda: ((c, EVERY, EVERY, EVERY), (1 - c, EVERY, EVERY, EVERY), self.device(c=1 - c)),
             }[stage]()
             out, back = [(True, copy(view(*mine), dev))], [(True, copy(view(*other), dev))]
-            return {'start': out, 'sent': out, 'recv': back}
+            start = [(use, copy(view(*mine), dev, src)) for use, src in first] or out
+            return {'start': start, 'sent': out, 'recv': back}
         hop = int(stage[1])
         ups, downs = (z >= hop - 1) & (z < 3), (z + hop <= 4) & (z > 0)
         above, below = self.device(z=jnp.minimum(z + 1, 3)), self.device(z=jnp.maximum(z - 1, 0))
@@ -97,8 +100,9 @@
             return [(one != other, copy(view(c, gx, gy, 0), above)), (one & other, copy(view(c, gx, gy, pl.ds(0, PAIR)), above))]
 
         return {
-            'start': [(ups, copy(view(c, gx, gy, jnp.maximum(z - hop + 1, 0)), above)),
-                      (downs, copy(view(c, gx, gy, jnp.minimum(z + hop - 1, 3)), below))],
+            'start': [(go & use, copy(view(c, gx, gy, z), to, src)) for go, to in ((ups, above), (downs, below)) for use, src in first]
+            or [(ups, copy(view(c, gx, gy, jnp.maximum(z - hop + 1, 0)), above)),
+                (downs, copy(view(c, gx, gy, jnp.minimum(z + hop - 1, 3)), below))],
             'sent': counted(ups, downs),
             'recv': counted(z >= hop, z + hop <= 3),
         }
@@ -144,6 +148,7 @@
                 for kind, is_kind in self.kinds(u):
                     @pl.when(is_kind)
                     def _(kind=kind):
+                        self.unit = u
                         self.advance(lax.rem(u + self.base, RING), kind, view(u), s)
 
 
@@ -353,7 +358,11 @@
                 piece_buf, dk_acc, dv_acc, s_buf, state, dkv_buf, peer_buf, gbuf, abuf, obuf, own_buf, oo_buf, w_buf, dn_buf, part_buf, z_parts, sum_buf, parts,
                 cs_send, cs_recv, send_sem, recv_sem, first_sem, proj_sem, rows_sem, do_send, do_recv,
                 lsem, gsem, asem, osem, tsend, trecv, psend, precv, rsem, wsem, gain_send, gain_recv):
-    net_in, net_cs, net = Gather(send_sem, recv_sem, (306463953, 1175604295)), Gather(cs_send, cs_recv, (306463953, 1175604295)), Gather(send_sem, recv_sem, (-398134202, 1293043604, -2075179916, 958350436), START)
+    def made(u):
+        rows = pl.ds(pl.multiple_of(lax.rem(u, N_IN) * ROWS_UNIT, ROWS_UNIT), ROWS_UNIT)
+        return [(u < N_IN, h_buf.at[rows, :]), (u >= N_IN, dy_ref.at[rows, :])]
+
+    net_in, net_cs, net = Gather(send_sem, recv_sem, (306463953, 1175604295), source=made), Gather(cs_send, cs_recv, (306463953, 1175604295)), Gather(send_sem, recv_sem, (-398134202, 1293043604, -2075179916, 958350436), START)
     quarter = net.y * 2 + net.x
     head = net.c * 4 + net.z
     spot = (net.y, net.x, net.c, net.z)
@@ -388,7 +397,6 @@
     first = [pltpu.make_async_copy(src, dst, first_sem.at[i]) for i, (src, dst) in enumerate((
         (h_buf, hd_ref.at[(0, *spot)]), (dy_ref, hd_ref.at[(1, *spot)]), (mypos_buf, pos_ref.at[spot])))]
     start_all(first)
-    wait_all(first)
     pl.semaphore_wait(barrier, TRIO + inner)
     q_cols = pl.ds(pl.multiple_of(head * TRIO * LANES, LANES), TRIO * LANES)
     kv_cols = pl.ds(pl.multiple_of(head * LANES, LANES), LANES)
@@ -689,6 +697,7 @@
 
         @pl.when(t == 1)
         def _():
+            wait_all(first)
             wo_rows(zero()).start()
             start_all(weights)
 
@@ -717,7 +726,7 @@
         net_in.tick(t, PAIR * N_IN, view_in)
         net.tick(t - START, N_UNIT, view)
         for s in range(N_STAGE + 2):
-            @pl.when(t == s * LAG)
+            @pl.when(t == s * LAG + 1)
             def _(s=s):
                 net_cs.advance(0, 'D', view_cs, s)
 

time: 552 us -> 550 us (level)
  no operation moved by 1% of the time
where the time goes in v6:
time: 550 us; the launch traced here: 549 us
  Pallas kernels  548 us (100%)
    pallas_call x1, Pallas kernels, main(): pl.pallas_call(main_kernel, out_shape=[like((PAIR, *GRID) + x.shape, BF16...  471 us
    pallas_call x1, Pallas kernels, finish(): pl.pallas_call(finish_kernel, out_shape=[like(x.shape, BF16), like(dx.sha...  77.4 us

profile of v6, /device:TPU:0, one launch (start us, length us, event | category | flops | bytes accessed | tf_op | source)
XLA Modules:
  0.0 549.2 jit_solution(7890079410333680655)
XLA Ops:
  0.6 471.0 %shard_map.144 = (bf16[2,2,2,2,4,128,3072]{6,5,4,3,2,1,0:T(8,128)(2,1)}, f32[2,2,2,4,8,128]{5,4,3,2,1,0:T(8,128)}, bf16[8,2,4,2,2,1024,128]{6,5,4,3,2,1,0:T(8,12...) custom-call(bf16[128,3072]{1,0:T(8,128)(2,1)} %x_ref.1, ...), custom_call_target="tpu_custom_call" | custom-call | tf_op jit(solution)/shard_map/pallas_call | solution.py:857
  471.6 77.4 %shard_map.145 = (bf16[128,3072]{1,0:T(8,128)(2,1)}, bf16[128,3072]{1,0:T(8,128)(2,1)}, f32[24,128]{1,0:T(8,128)}, f32[3072,3072]{1,0:T(8,128)}, f32[3072,1024]{...) custom-call(f32[128,3072]{1,0:T(8,128)} %get-tuple-element.21.sum_ref, ...), custom_call_target="tpu_custom_call" | custom-call | flops 51539607552 | bytes 262144000 | tf_op jit(solution)/shard_map/pallas_call | solution.py:1008
